TPU v7x, 32 devices: a 4x4x1 block of a 4x4x8 slice. The times are simulated.
32 devices in a mesh: dp: 1 (over z), tp: 4 (over y), fsdp: 4 (over x), cp: 2 (over core).
Axes of the slice: x: 4, y: 4, z: 1, core: 2. Of those that a mesh axis runs over, the one named last changes fastest.
The devices are a block of a 4x4x8 slice.
Arguments:
- hidden: bfloat16 [12, 1536, 4096], P(('dp', 'fsdp'), 'cp')
- positions: int32 [12, 1536], P(('dp', 'fsdp'), 'cp')
- attn_gain: float32 [4096], replicated
- w_query: bfloat16 [4096, 32, 128], P(('fsdp', 'cp'), 'tp')
- w_key: bfloat16 [4096, 8, 128], P(('fsdp', 'cp'), 'tp')
- w_value: bfloat16 [4096, 8, 128], P(('fsdp', 'cp'), 'tp')
- w_out: bfloat16 [32, 128, 4096], P('tp', None, ('fsdp', 'cp'))
- mlp_gain: float32 [4096], replicated
- w_gate: bfloat16 [4096, 14336], P(('fsdp', 'cp'), 'tp')
- w_up: bfloat16 [4096, 14336], P(('fsdp', 'cp'), 'tp')
- w_down: bfloat16 [14336, 4096], P('tp', ('fsdp', 'cp'))
Outputs:
- output: bfloat16 [12, 1536, 4096], P(('dp', 'fsdp'), 'cp')
All inputs are finite; a program needn't handle non-finite values.
Results may differ from a plain program's by a relative error of at most 0.0135401.
Values are sent between devices in bfloat16 or wider.
A program may use at most 768 MiB of HBM per device.

v0:
```python
import functools
import math

import jax
import jax.numpy as jnp
from jax import lax
from jax.experimental import pallas as pl
from jax.experimental.pallas import tpu as pltpu
from jax.sharding import PartitionSpec as P


ROPE_THETA = 500000.0
NORM_EPS = 1e-5
GROUP_AXES = ('fsdp', 'cp')
VMEM_LIMIT = 62 * 1024 * 1024
F32 = jnp.float32
BF16 = jnp.bfloat16
MESH = pl.DeviceIdType.MESH
ANY = pl.BlockSpec(memory_space=pl.ANY)
VMEM = pl.BlockSpec(memory_space=pltpu.VMEM)


def rms_norm(hidden_f32, gain):
    mean_sq = jnp.mean(hidden_f32 * hidden_f32, axis=-1, keepdims=True)
    return (hidden_f32 * lax.rsqrt(mean_sq + NORM_EPS) * gain).astype(BF16)


def cost(flops, bytes_accessed):
    return pl.CostEstimate(flops=int(flops), bytes_accessed=int(bytes_accessed), transcendentals=0)


def proj_kernel(rope_heads, head, x_ref, w_ref, cos_ref, sin_ref, o_ref):
    acc = jnp.dot(x_ref[...], w_ref[...], preferred_element_type=F32)
    cos, sin = cos_ref[...], sin_ref[...]
    for i in range(acc.shape[1] // head):
        part = acc[:, i * head:(i + 1) * head]
        if i < rope_heads:
            part = part * cos + pltpu.roll(part, head // 2, 1) * sin
        o_ref[:, i * head:(i + 1) * head] = part.astype(BF16)


def project(x, w, cos, sin, col_block, width, rope_heads, head, tile=256):
    rows, depth = x.shape
    tile = math.gcd(tile, rows)
    return pl.pallas_call(
        functools.partial(proj_kernel, rope_heads, head),
        grid=(rows // tile,),
        in_specs=[
            pl.BlockSpec((tile, depth), lambda i: (i, 0)),
            pl.BlockSpec((depth, width), lambda i: (0, col_block)),
            pl.BlockSpec((tile, head), lambda i: (i, 0)),
            pl.BlockSpec((tile, head), lambda i: (i, 0)),
        ],
        out_specs=pl.BlockSpec((tile, width), lambda i: (i, 0)),
        out_shape=jax.ShapeDtypeStruct((rows, width), BF16),
        compiler_params=pltpu.CompilerParams(vmem_limit_bytes=VMEM_LIMIT),
        cost_estimate=cost(2 * rows * depth * width, 2 * (rows * depth + depth * width + rows * width)),
    )(x, w, cos, sin)


def attn_kernel(group, head, seg, q_ref, ko_ref, vo_ref, kp_ref, vp_ref, o_ref):
    c = lax.axis_index('cp')
    scale = head ** -0.5 * math.log2(math.e)

    def run(first_full, second_full):
        low, high = pl.ds(0, seg), pl.ds(seg, seg)
        own_low, own_high = (ko_ref, vo_ref, low), (ko_ref, vo_ref, high)
        tri = lax.broadcasted_iota(jnp.int32, (seg, seg), 0) >= lax.broadcasted_iota(jnp.int32, (seg, seg), 1)
        for g in range(group):
            cols = pl.ds(g * head, head)
            for rows, diag, full in ((low, own_low, first_full), (high, own_high, second_full)):
                q = q_ref[rows, cols]
                blocks = full + [diag]
                scores = []
                for k_ref, _, part in blocks:
                    scores.append(lax.dot_general(q, k_ref[part, :], (((1,), (1,)), ((), ())), preferred_element_type=F32))
                scores[-1] = jnp.where(tri, scores[-1], -jnp.inf)
                top = functools.reduce(jnp.maximum, [jnp.max(s, axis=-1, keepdims=True) for s in scores])
                total = jnp.zeros((seg, 1), F32)
                out = jnp.zeros((seg, head), F32)
                for s, (_, v_ref, part) in zip(scores, blocks):
                    p = jnp.exp2((s - top) * scale)
                    total = total + jnp.sum(p, axis=-1, keepdims=True)
                    out = out + jnp.dot(p.astype(BF16), v_ref[part, :], preferred_element_type=F32)
                o_ref[rows, cols] = (out / total).astype(BF16)

    low, high = pl.ds(0, seg), pl.ds(seg, seg)
    own_low, peer_low, peer_high = (ko_ref, vo_ref, low), (kp_ref, vp_ref, low), (kp_ref, vp_ref, high)

    @pl.when(c == 0)
    def _():
        run([], [own_low, peer_low, peer_high])

    @pl.when(c == 1)
    def _():
        run([peer_low], [peer_low, own_low])


def attention(q, kv_own, kv_peer, n_seqs, kv_heads, group, head):
    rows = q.shape[0]
    tokens = rows // n_seqs
    q_spec = pl.BlockSpec((tokens, group * head), lambda i, h: (i, h))
    k_spec = pl.BlockSpec((tokens, head), lambda i, h: (i, h))
    v_spec = pl.BlockSpec((tokens, head), lambda i, h: (i, kv_heads + h))
    return pl.pallas_call(
        functools.partial(attn_kernel, group, head, tokens // 2),
        grid=(n_seqs, kv_heads),
        in_specs=[q_spec, k_spec, v_spec, k_spec, v_spec],
        out_specs=q_spec,
        out_shape=jax.ShapeDtypeStruct(q.shape, BF16),
        compiler_params=pltpu.CompilerParams(vmem_limit_bytes=VMEM_LIMIT),
        cost_estimate=cost(10 * rows * tokens * kv_heads * group * head, 4 * q.size),
    )(q, kv_own, kv_own, kv_peer, kv_peer)


def ring_barrier(right, left):
    barrier = pltpu.get_barrier_semaphore()
    for neighbour in (right, left):
        pl.semaphore_signal(barrier, inc=1, device_id={'tp': neighbour}, device_id_type=MESH)
    pl.semaphore_wait(barrier, 2)


def ring_place(n):
    me = lax.axis_index('tp')
    return me, lax.rem(me + 1, n), lax.rem(me + n - 1, n)


def shard_of(me, direction, back, n):
    return lax.rem(me + (n - back if direction == 0 else back), n)


def ring_matmul_scatter(n, me, sides, u_refs, w_ref, u_buf, w_buf, s_buf, r_buf, u_sem, w_sem, send_sem, recv_sem, finish):
    half = u_buf.shape[2]
    block = w_buf.shape[2]
    blocks = w_ref.shape[1] // block

    def u_copies(step):
        copies = []
        for d in range(2):
            row = pl.multiple_of(shard_of(me, d, step + 1, n) * (2 * half) + d * half, 16)
            at = 0
            for i, u_ref in enumerate(u_refs):
                copies.append(pltpu.make_async_copy(
                    u_ref.at[pl.ds(row, half), :], u_buf.at[step % 2, d, :, pl.ds(at, u_ref.shape[1])], u_sem.at[step % 2, d, i]))
                at += u_ref.shape[1]
        return copies

    def w_copy(cb, slot):
        return pltpu.make_async_copy(w_ref.at[:, pl.ds(pl.multiple_of(cb * block, block), block)], w_buf.at[slot], w_sem.at[slot])

    def send(step, d, cb):
        src = s_buf.at[d, cb] if step == 0 else r_buf.at[step - 1, d, cb]
        return pltpu.make_async_remote_copy(
            src_ref=src, dst_ref=r_buf.at[step, d, cb], send_sem=send_sem.at[step, d, cb], recv_sem=recv_sem.at[step, d, cb],
            device_id={'tp': sides[d]}, device_id_type=MESH)

    for c in u_copies(0):
        c.start()
    w_copy(0, 0).start()
    for step in range(n):
        for c in u_copies(step):
            c.wait()
        if step + 1 < n:
            for c in u_copies(step + 1):
                c.start()

        def one_block(cb, _, step=step):
            slot = lax.rem(cb, 2)
            w_copy(cb, slot).wait()
            if step + 1 < n:
                w_copy(lax.rem(cb + 1, blocks), 1 - slot).start()
            else:
                @pl.when(cb + 1 < blocks)
                def _():
                    w_copy(cb + 1, 1 - slot).start()
            parts = [jnp.dot(u_buf[step % 2, d], w_buf[slot], preferred_element_type=F32) for d in range(2)]
            for d in range(2):
                part = parts[d]
                if step > 0:
                    send(step - 1, d, cb).wait_recv()
                    part = part + r_buf[step - 1, d, cb].astype(F32)
                if step + 1 < n:
                    if step == 0:
                        s_buf[d, cb] = part.astype(BF16)
                    else:
                        r_buf[step - 1, d, cb] = part.astype(BF16)
                    send(step, d, cb).start()
                else:
                    finish(d, cb, part)
            return 0

        lax.fori_loop(0, blocks, one_block, 0)

    def drain(cb, _):
        for step in range(n - 1):
            for d in range(2):
                send(step, d, cb).wait_send()
        return 0

    lax.fori_loop(0, blocks, drain, 0)


def ring_scratch(n, half, depth, block, blocks, n_u):
    return [
        pltpu.VMEM((2, 2, half, depth), BF16),
        pltpu.VMEM((2, depth, block), BF16),
        pltpu.VMEM((2, blocks, half, block), BF16),
        pltpu.VMEM((n - 1, 2, blocks, half, block), BF16),
        pltpu.SemaphoreType.DMA((2, 2, n_u)),
        pltpu.SemaphoreType.DMA((2,)),
        pltpu.SemaphoreType.DMA((n - 1, 2, blocks)),
        pltpu.SemaphoreType.DMA((n - 1, 2, blocks)),
    ]


def out_kernel(n, o_ref, w_ref, h_ref, gain_ref, r_ref, b_ref, h_buf, h_sem, u_buf, w_buf, s_buf, r_buf, u_sem, w_sem, send_sem, recv_sem):
    me, right, left = ring_place(n)
    shard, _ = r_ref.shape
    half = shard // 2
    block = w_buf.shape[2]
    load_h = pltpu.make_async_copy(h_ref.at[pl.ds(pl.multiple_of(me * shard, 16), shard), :], h_buf, h_sem)
    load_h.start()
    ring_barrier(right, left)
    load_h.wait()

    def finish(d, cb, part):
        rows, cols = pl.ds(d * half, half), pl.ds(pl.multiple_of(cb * block, block), block)
        total = h_buf[rows, cols].astype(F32) + part.astype(BF16).astype(F32)
        r_ref[rows, cols] = total.astype(BF16)

    ring_matmul_scatter(n, me, (right, left), [o_ref], w_ref, u_buf, w_buf, s_buf, r_buf, u_sem, w_sem, send_sem, recv_sem, finish)
    gain = gain_ref[...]

    def norm_rows(i, _):
        rows = pl.ds(pl.multiple_of(i * 16, 16), 16)
        b_ref[rows, :] = rms_norm(r_ref[rows, :].astype(F32), gain)
        return 0

    lax.fori_loop(0, shard // 16, norm_rows, 0)


def out_project(n, mixed, w_out, hidden, gain):
    rows, depth = mixed.shape
    width = w_out.shape[1]
    shard = rows // n
    block = min(512, width // 2)
    blocks = width // block
    return pl.pallas_call(
        functools.partial(out_kernel, n),
        in_specs=[ANY, ANY, ANY, VMEM],
        out_specs=[VMEM, VMEM],
        out_shape=[jax.ShapeDtypeStruct((shard, width), BF16)] * 2,
        scratch_shapes=[pltpu.VMEM((shard, width), BF16), pltpu.SemaphoreType.DMA]
        + ring_scratch(n, shard // 2, depth, block, blocks, 1),
        compiler_params=pltpu.CompilerParams(collective_id=0, has_side_effects=True, vmem_limit_bytes=VMEM_LIMIT),
        cost_estimate=cost(2 * rows * depth * width * 5, 2 * (rows * depth + depth * width)),
    )(mixed, w_out, hidden, gain)


def gated(x, w_gate, w_up):
    gate = jnp.dot(x, w_gate, preferred_element_type=F32)
    up = jnp.dot(x, w_up, preferred_element_type=F32)
    return (jax.nn.silu(gate) * up).astype(BF16)


def gather_gate_kernel(n, pieces, b_ref, w_ref, all_ref, u_ref, w_buf, x_buf, u_buf, w_sem, x_sem, own_sem, u_sem, send_sem, recv_sem):
    me, right, left = ring_place(n)
    sides = (right, left)
    shard = b_ref.shape[0]
    half = shard // 2
    piece = half // pieces
    ff = u_ref.shape[1]
    tile = min(256, ff)
    tiles = ff // tile

    def w_copies(t):
        out = []
        for i in range(2):
            cols = pl.ds(pl.multiple_of(i * ff + t * tile, tile), tile)
            out.append(pltpu.make_async_copy(w_ref.at[:, cols], w_buf.at[:, cols], w_sem.at[t, i]))
        return out

    def rows_of(d, back, j):
        return pl.ds(pl.multiple_of(shard_of(me, d, back, n) * shard + d * half + j * piece, 16), piece)

    def hop(a, d, j):
        rows = rows_of(d, a, j)
        src = b_ref.at[pl.ds(d * half + j * piece, piece), :] if a == 0 else all_ref.at[rows, :]
        return pltpu.make_async_remote_copy(
            src_ref=src, dst_ref=all_ref.at[rows, :], send_sem=send_sem.at[a, d, j], recv_sem=recv_sem.at[a, d, j],
            device_id={'tp': sides[d]}, device_id_type=MESH)

    def arrival(a, d, j):
        rows = rows_of(d, a + 1, j)
        return pltpu.make_async_remote_copy(
            src_ref=all_ref.at[rows, :], dst_ref=all_ref.at[rows, :], send_sem=send_sem.at[a, d, j], recv_sem=recv_sem.at[a, d, j],
            device_id={'tp': sides[d]}, device_id_type=MESH)

    def x_copies(a):
        return [pltpu.make_async_copy(
            all_ref.at[pl.ds(pl.multiple_of(shard_of(me, d, a, n) * shard + d * half, 16), half), :],
            x_buf.at[a % 2, pl.ds(d * half, half), :], x_sem.at[a % 2, d]) for d in range(2)]

    def u_copies(a):
        return [pltpu.make_async_copy(
            u_buf.at[a % 2, pl.ds(d * half, half), :],
            u_ref.at[pl.ds(pl.multiple_of(shard_of(me, d, a, n) * shard + d * half, 16), half), :], u_sem.at[a % 2, d]) for d in range(2)]

    load_own = pltpu.make_async_copy(b_ref, x_buf.at[0], x_sem.at[0, 0])
    load_own.start()

    def load_w(t, _):
        for c in w_copies(t):
            c.start()
        return 0

    lax.fori_loop(0, tiles, load_w, 0)
    ring_barrier(right, left)
    for j in range(pieces):
        for d in range(2):
            hop(0, d, j).start()
    load_own.wait()
    keep_own = pltpu.make_async_copy(x_buf.at[0], all_ref.at[pl.ds(pl.multiple_of(me * shard, 16), shard), :], own_sem)
    keep_own.start()
    for a in range(n):
        if a > 0:
            for j in range(pieces):
                for d in range(2):
                    arrival(a - 1, d, j).wait_recv()
                    if a + 1 < n:
                        hop(a, d, j).start()
            if a == 2:
                keep_own.wait()
            for c in x_copies(a):
                c.start()
            for c in x_copies(a):
                c.wait()
        if a >= 2:
            for c in u_copies(a - 2):
                c.wait()

        def one_tile(t, _, a=a):
            if a == 0:
                for c in w_copies(t):
                    c.wait()
            at = pl.multiple_of(t * tile, tile)
            u_buf[a % 2, :, pl.ds(at, tile)] = gated(x_buf[a % 2], w_buf[:, pl.ds(at, tile)], w_buf[:, pl.ds(ff + at, tile)])
            return 0

        lax.fori_loop(0, tiles, one_tile, 0)
        for c in u_copies(a):
            c.start()
    for a in range(max(0, n - 2), n):
        for c in u_copies(a):
            c.wait()
    for a in range(n - 1):
        for j in range(pieces):
            for d in range(2):
                hop(a, d, j).wait_send()


def gather_gate(n, b, w):
    shard, depth = b.shape
    ff = w.shape[1] // 2
    tiles = ff // min(256, ff)
    pieces = 3
    rows = shard * n
    return pl.pallas_call(
        functools.partial(gather_gate_kernel, n, pieces),
        in_specs=[ANY, ANY],
        out_specs=[ANY, ANY],
        out_shape=[jax.ShapeDtypeStruct((rows, depth), BF16), jax.ShapeDtypeStruct((rows, ff), BF16)],
        scratch_shapes=[
            pltpu.VMEM((depth, 2 * ff), BF16),
            pltpu.VMEM((2, shard, depth), BF16),
            pltpu.VMEM((2, shard, ff), BF16),
            pltpu.SemaphoreType.DMA((tiles, 2)),
            pltpu.SemaphoreType.DMA((2, 2)),
            pltpu.SemaphoreType.DMA,
            pltpu.SemaphoreType.DMA((2, 2)),
            pltpu.SemaphoreType.DMA((n - 1, 2, pieces)),
            pltpu.SemaphoreType.DMA((n - 1, 2, pieces)),
        ],
        compiler_params=pltpu.CompilerParams(collective_id=1, has_side_effects=True, vmem_limit_bytes=VMEM_LIMIT),
        cost_estimate=cost(4 * rows * depth * ff * 2, 2 * rows * depth + 2 * w.size),
    )(b, w)


def gate_kernel(x_ref, g_ref, u_ref, o_ref):
    o_ref[...] = gated(x_ref[...], g_ref[...], u_ref[...])


def gate_up(x, w, tile_rows):
    rows, depth = x.shape
    ff = w.shape[1] // 2
    tile = min(256, ff)
    return pl.pallas_call(
        gate_kernel,
        grid=(rows // tile_rows, ff // tile),
        in_specs=[
            pl.BlockSpec((tile_rows, depth), lambda i, j: (i, 0)),
            pl.BlockSpec((depth, tile), lambda i, j: (0, j)),
            pl.BlockSpec((depth, tile), lambda i, j: (0, ff // tile + j)),
        ],
        out_specs=pl.BlockSpec((tile_rows, tile), lambda i, j: (i, j)),
        out_shape=jax.ShapeDtypeStruct((rows, ff), BF16),
        compiler_params=pltpu.CompilerParams(vmem_limit_bytes=VMEM_LIMIT),
        cost_estimate=cost(4 * rows * depth * ff, 2 * rows * depth + 2 * w.size),
    )(x, w, w)


def down_kernel(n, ua_ref, ub_ref, w_ref, r_ref, y_ref, res_buf, res_sem, own_sem, ag_send, ag_recv,
                u_buf, w_buf, s_buf, r_buf, u_sem, w_sem, send_sem, recv_sem):
    me, right, left = ring_place(n)
    sides = (right, left)
    shard = r_ref.shape[0]
    half = shard // 2
    block = w_buf.shape[2]
    blocks = w_ref.shape[1] // block
    load_r = pltpu.make_async_copy(r_ref, res_buf, res_sem)
    load_r.start()
    ring_barrier(right, left)
    load_r.wait()

    def place(d, back, cb):
        row = pl.multiple_of(shard_of(me, d, back, n) * shard + d * half, 16)
        return y_ref.at[pl.ds(row, half), pl.ds(pl.multiple_of(cb * block, block), block)]

    def hop(a, d, cb):
        src = r_buf.at[n - 2, d, cb] if a == 0 else place(d, a, cb)
        return pltpu.make_async_remote_copy(
            src_ref=src, dst_ref=place(d, a, cb), send_sem=ag_send.at[a, d, cb], recv_sem=ag_recv.at[a, d, cb],
            device_id={'tp': sides[d]}, device_id_type=MESH)

    def arrival(a, d, cb):
        return pltpu.make_async_remote_copy(
            src_ref=place(d, a + 1, cb), dst_ref=place(d, a + 1, cb), send_sem=ag_send.at[a, d, cb], recv_sem=ag_recv.at[a, d, cb],
            device_id={'tp': sides[d]}, device_id_type=MESH)

    def keep(d, cb):
        return pltpu.make_async_copy(r_buf.at[n - 2, d, cb], place(d, 0, cb), own_sem.at[d, cb])

    def finish(d, cb, part):
        rows, cols = pl.ds(d * half, half), pl.ds(pl.multiple_of(cb * block, block), block)
        total = res_buf[rows, cols].astype(F32) + part.astype(BF16).astype(F32)
        r_buf[n - 2, d, cb] = total.astype(BF16)
        hop(0, d, cb).start()
        keep(d, cb).start()

    ring_matmul_scatter(n, me, sides, [ua_ref, ub_ref], w_ref, u_buf, w_buf, s_buf, r_buf, u_sem, w_sem, send_sem, recv_sem, finish)
    for a in range(n - 1):
        def forward(cb, _, a=a):
            for d in range(2):
                arrival(a, d, cb).wait_recv()
                if a + 1 < n - 1:
                    hop(a + 1, d, cb).start()
            return 0

        lax.fori_loop(0, blocks, forward, 0)

    def drain(cb, _):
        for d in range(2):
            keep(d, cb).wait()
            for a in range(n - 1):
                hop(a, d, cb).wait_send()
        return 0

    lax.fori_loop(0, blocks, drain, 0)


def down_project(n, act_a, act_b, w_down, resid):
    rows = act_a.shape[0]
    depth, width = w_down.shape
    shard = rows // n
    block = min(512, width // 2)
    blocks = width // block
    return pl.pallas_call(
        functools.partial(down_kernel, n),
        in_specs=[ANY, ANY, ANY, ANY],
        out_specs=ANY,
        out_shape=jax.ShapeDtypeStruct((rows, width), BF16),
        scratch_shapes=[
            pltpu.VMEM((shard, width), BF16), pltpu.SemaphoreType.DMA, pltpu.SemaphoreType.DMA((2, blocks)),
            pltpu.SemaphoreType.DMA((n - 1, 2, blocks)), pltpu.SemaphoreType.DMA((n - 1, 2, blocks)),
        ] + ring_scratch(n, shard // 2, depth, block, blocks, 2),
        compiler_params=pltpu.CompilerParams(collective_id=2, has_side_effects=True, vmem_limit_bytes=VMEM_LIMIT),
        cost_estimate=cost(2 * rows * depth * width * 4, 2 * (rows * depth + depth * width)),
    )(act_a, act_b, w_down, resid)


def gather(shard, axis):
    return lax.all_gather(shard, GROUP_AXES, axis=axis, tiled=True)


def solution(mesh):
    n_tp = mesh.shape['tp']
    assert mesh.shape['cp'] == 2
    seq_spec = P(('dp', 'fsdp'), 'cp', None)
    pos_spec = P(('dp', 'fsdp'), 'cp')
    in_spec = P(GROUP_AXES, 'tp', None)
    out_spec = P('tp', None, GROUP_AXES)
    col_spec = P(GROUP_AXES, 'tp')
    row_spec = P('tp', GROUP_AXES)
    rep_spec = P(None)

    def layer_local(hidden, positions, attn_gain, w_query, w_key, w_value, w_out, mlp_gain, w_gate, w_up, w_down):
        n_seqs, tokens, d_model = hidden.shape
        heads, head = w_query.shape[1:]
        kv_heads = w_key.shape[1]
        rows = n_seqs * tokens
        local = w_query.shape[0]
        ff_half = w_gate.shape[1] // 2
        x = hidden.reshape(rows, d_model)

        w_qkv = jnp.concatenate([w.reshape(local, -1) for w in (w_query, w_key, w_value)], axis=1)
        full_qkv = gather(w_qkv, 0)
        full_out = gather(w_out.reshape(heads * head, -1), 1)
        full_a = gather(jnp.concatenate([w_gate[:, :ff_half], w_up[:, :ff_half]], axis=1), 0)
        full_b = gather(jnp.concatenate([w_gate[:, ff_half:], w_up[:, ff_half:]], axis=1), 0)
        full_down = gather(w_down, 1)

        normed = rms_norm(x.astype(F32), attn_gain)
        inv_freq = ROPE_THETA ** (-jnp.arange(0, head, 2, dtype=F32) / head)
        angles = positions.reshape(rows, 1).astype(F32) * inv_freq
        cos, sin = jnp.cos(angles), jnp.sin(angles)
        cos = jnp.concatenate([cos, cos], axis=1)
        sin = jnp.concatenate([-sin, sin], axis=1)

        q_width, kv_width = heads * head, 2 * kv_heads * head
        kv = project(normed, full_qkv, cos, sin, q_width // kv_width, kv_width, kv_heads, head)
        kv_peer = lax.ppermute(kv, 'cp', [(0, 1), (1, 0)])
        q = project(normed, full_qkv, cos, sin, 0, q_width, heads, head)
        mixed = attention(q, kv, kv_peer, n_seqs, kv_heads, heads // kv_heads, head)
        resid, normed_mlp = out_project(n_tp, mixed, full_out, x, mlp_gain.reshape(1, d_model))
        all_normed, act_a = gather_gate(n_tp, normed_mlp, full_a)
        act_b = gate_up(all_normed, full_b, rows // n_tp)
        y = down_project(n_tp, act_a, act_b, full_down, resid)
        return y.reshape(hidden.shape)

    return jax.shard_map(
        layer_local, mesh=mesh,
        in_specs=(seq_spec, pos_spec, rep_spec, in_spec, in_spec, in_spec, out_spec, rep_spec, col_spec, col_spec, row_spec),
        out_specs=seq_spec, check_vma=False)
```

profile of v0, /device:TPU:97, one launch (start us, length us, event | category | flops | bytes accessed | tf_op | source)
XLA Modules:
  0.0 923.8 jit_solution(9345329815005393254)
XLA Ops:
  6.5 0.0 all-gather.6.cloned.1.call-start
  6.6 1.5 copy.18
  8.0 1.1 copy_bitcast_fusion.1
  9.2 1.3 pad_maximum_fusion.2
  10.4 0.1 all-gather.6.cloned.1.call-update
  10.5 0.1 all-gather.8.cloned.1.call-start
  10.6 0.7 all-gather.8.cloned.1.call-update
  11.3 0.1 all-gather.10.cloned.1.call-start
  11.4 4.9 fusion.1
  16.2 2.2 pad_maximum_fusion
  18.4 0.1 all-gather.10.cloned.1.call-update
  18.5 0.1 all-gather.12.cloned.1.call-start
  18.6 3.6 pad_maximum_fusion.1
  22.2 0.0 copy-start.1
  22.2 0.1 all-gather.12.cloned.1.call-update
  22.2 0.1 all-gather.14.cloned.1.call-start
  22.3 0.6 all-gather.14.cloned.1.call-update
  22.9 0.0 copy-done.1
  22.9 9.1 multiply_reduce_fusion
  32.1 4.2 fusion
  36.2 0.0 copy-start
  36.3 2.1 pad_maximum_fusion.3
  38.4 0.0 copy-done
  38.4 18.7 %multiply_convert_fusion.x_ref = bf16[2304,4096]{1,0:T(8,128)(2,1)} fusion(f32[4096]{0:T(1024)S(1)} %copy-done, f32[2304]{0:T(1024)S(1)} %rsqrt.12, bf16[3,768,4096]{2,1,0:T(8,128)(2,1)} %param.11), kind=kLoop, calls=%fused_computation | loop fusion | flops 37748736 | bytes 37774336 | tf_op jit(solution)/shard_map/convert_element_type | solution.py:25
  57.1 22.6 %all-gather.6.cloned.1.call-done.w_ref = bf16[4096,1536]{1,0:T(8,128)(2,1)} async-done(((bf16[512,1536]{1,0:T(8,128)(2,1)}), bf16[4096,1536]{1,0:T(8,128)(2,1)}) %all-gather.6.cloned.1.call-update) | async-done | bytes 12582928 | tf_op jit(solution)/shard_map/all_gather | solution.py:492
  79.7 17.8 %shard_map.110.ko_ref.vo_ref = bf16[2304,512]{1,0:T(8,128)(2,1)} custom-call(bf16[2304,4096]{1,0:T(8,128)(2,1)} %multiply_convert_fusion.x_ref, bf16[4096,1536]{1,0:T(8,128)(2,1)} %all-gather.6.cloned.1.call-done.w_ref, f32[2304,128]{1,0:T(8,128)} %get-tuple-element.22.cos_ref, f32[2304,128]{1,0:T(8,128)} %get-tuple-element.23.sin_ref), custom_call_target="tpu_custom_call" | custom-call | flops 9663676416 | bytes 25427968 | tf_op jit(solution)/shard_map/pallas_call | solution.py:45
  97.5 0.2 collective-permute-start
  97.8 27.6 %shard_map.109.q_ref = bf16[2304,1024]{1,0:T(8,128)(2,1)} custom-call(bf16[2304,4096]{1,0:T(8,128)(2,1)} %multiply_convert_fusion.x_ref, bf16[4096,1536]{1,0:T(8,128)(2,1)} %all-gather.6.cloned.1.call-done.w_ref, f32[2304,128]{1,0:T(8,128)} %get-tuple-element.22.cos_ref, f32[2304,128]{1,0:T(8,128)} %get-tuple-element.23.sin_ref), custom_call_target="tpu_custom_call" | custom-call | flops 19327352832 | bytes 31981568 | tf_op jit(solution)/shard_map/pallas_call | solution.py:45
  125.4 0.0 collective-permute-done.kp_ref.vp_ref
  125.4 31.9 %shard_map.111.o_ref = bf16[2304,1024]{1,0:T(8,128)(2,1)} custom-call(bf16[2304,1024]{1,0:T(8,128)(2,1)} %shard_map.109.q_ref, bf16[2304,512]{1,0:T(8,128)(2,1)} %shard_map.110.ko_ref.vo_ref, bf16[2304,512]{1,0:T(8,128)(2,1)} %shard_map.110.ko_ref.vo_ref, bf16[2304,512]{1,0:T(8,128)(2,1)} %collective-permute-done.kp_ref.vp_ref, ...), custom_call_target="tpu_custom_call" | custom-call | flops 18119393280 | bytes 9437184 | tf_op jit(solution)/shard_map/pallas_call | solution.py:105
  157.2 0.0 all-gather.8.cloned.1.call-done.w_ref
  157.2 171.1 %shard_map.112 = (bf16[576,4096]{1,0:T(8,128)(2,1)}, bf16[576,4096]{1,0:T(8,128)(2,1)}) custom-call(bf16[2304,1024]{1,0:T(8,128)(2,1)} %shard_map.111.o_ref, bf16[1024,4096]{1,0:T(8,128)(2,1)} %all-gather.8.cloned.1.call-done.w_ref, bf16[2304,4096]{1,0:T(8,128)(2,1)} %bitcast.15, f32[1,4096]{1,0:T(1,128)} %bitcast.22), custom_call_target="tpu_custom_call" | custom-call | flops 96636764160 | bytes 13107200 | tf_op jit(solution)/shard_map/pallas_call | solution.py:248
  328.3 0.0 all-gather.10.cloned.1.call-done.w_ref
  328.4 176.9 %shard_map.113 = (bf16[2304,4096]{1,0:T(8,128)(2,1)}, bf16[2304,1792]{1,0:T(8,128)(2,1)}) custom-call(bf16[576,4096]{1,0:T(8,128)(2,1)} %get-tuple-element.9.b_ref, bf16[4096,3584]{1,0:T(8,128)(2,1)} %all-gather.10.cloned.1.call-done.w_ref), custom_call_target="tpu_custom_call" | custom-call | flops 135291469824 | bytes 48234496 | tf_op jit(solution)/shard_map/pallas_call | solution.py:368
  505.2 0.0 all-gather.12.cloned.1.call-done.g_ref.u_ref
  505.3 81.9 %shard_map.114.ub_ref = bf16[2304,1792]{1,0:T(8,128)(2,1)} custom-call(bf16[2304,4096]{1,0:T(8,128)(2,1)} %get-tuple-element.11.x_ref, bf16[4096,3584]{1,0:T(8,128)(2,1)} %all-gather.12.cloned.1.call-done.g_ref.u_ref, bf16[4096,3584]{1,0:T(8,128)(2,1)} %all-gather.12.cloned.1.call-done.g_ref.u_ref), custom_call_target="tpu_custom_call" | custom-call | flops 67645734912 | bytes 48234496 | tf_op jit(solution)/shard_map/pallas_call | solution.py:397
  587.1 0.0 all-gather.14.cloned.1.call-done.w_ref
  587.1 313.1 %shard_map.115 = bf16[2304,4096]{1,0:T(8,128)(2,1)} custom-call(bf16[2304,1792]{1,0:T(8,128)(2,1)} %get-tuple-element.10.ua_ref, bf16[2304,1792]{1,0:T(8,128)(2,1)} %shard_map.114.ub_ref, bf16[3584,4096]{1,0:T(8,128)(2,1)} %all-gather.14.cloned.1.call-done.w_ref, bf16[576,4096]{1,0:T(8,128)(2,1)} %get-tuple-element.12.r_ref), custom_call_target="tpu_custom_call" | custom-call | flops 270582939648 | bytes 45875200 | tf_op jit(solution)/shard_map/pallas_call | solution.py:477
  900.2 16.8 %copy.20 = bf16[3,768,4096]{2,1,0:T(8,128)(2,1)} copy(bf16[3,768,4096]{2,1,0:T(8,128)(2,1)} %bitcast.16) | data formatting | bytes 37748736
  (5 shorter events, 0.0 us)
Async XLA Ops:
  6.5 73.2 %all-gather.6.cloned.1.call-start = ((), (), s32[]{:S(2)}) async-start(), calls=%async_computation | async-start | bytes 14155776 | tf_op jit(solution)/shard_map/all_gather | solution.py:492
  10.5 146.7 %all-gather.8.cloned.1.call-start = ((), (), s32[]{:S(2)}) async-start(), calls=%async_computation.1 | async-start | bytes 9437184 | tf_op jit(solution)/shard_map/all_gather | solution.py:492
  11.3 317.0 %all-gather.10.cloned.1.call-start = ((), (), s32[]{:S(2)}) async-start(), calls=%async_computation.2 | async-start | bytes 33030144 | tf_op jit(solution)/shard_map/all_gather | solution.py:492
  18.5 486.8 %all-gather.12.cloned.1.call-start = ((), (), s32[]{:S(2)}) async-start(), calls=%async_computation.3 | async-start | bytes 33030144 | tf_op jit(solution)/shard_map/all_gather | solution.py:492
  22.2 0.7 copy-start.1
  22.2 564.9 %all-gather.14.cloned.1.call-start = ((), (), s32[]{:S(2)}) async-start(), calls=%async_computation.4 | async-start | bytes 33030144 | tf_op jit(solution)/shard_map/all_gather | solution.py:492
  36.2 2.1 copy-start
  97.5 27.8 %collective-permute-start = (bf16[2304,512]{1,0:T(8,128)(2,1)}, bf16[2304,512]{1,0:T(8,128)(2,1)}, u32[]{:S(2)}, u32[]{:S(2)}) collective-permute-start(bf16[2304,512]{1,0:T(8,128)(2,1)} %shard_map.110.ko_ref.vo_ref), channel_id=1, source_target_pairs={{0,1},{1,0},{2,3},{3,2},{4,5},{5,4},{6,7},{7,6},{8,9},{9,8},{10,11... | collective-permute-start | bytes 7077896 | tf_op jit(solution)/shard_map/ppermute | solution.py:531
Sparse Core Ops, SparseCore 0:
  10.6 69.0 all-gather.5
  81.3 47.4 all-gather.7
  130.4 135.6 all-gather.9
  267.5 136.4 all-gather.11
  405.5 136.4 all-gather.13
where the time goes:
time: 934 us; the launch traced here: 924 us
  Pallas kernels  820 us (88%)
  other arithmetic  41.2 us (4%)
  local copies, waits for them, and re-layouts  24.3 us (3%)
  waiting for transfers between devices  24.2 us (3%)
  between operations  13.5 us (1%)
    pallas_call x1, Pallas kernels, down_project(): pl.pallas_call(functools.partial(down_kernel, n), in_specs=[ANY, ANY, ANY...  313 us
    pallas_call x1, Pallas kernels, gather_gate(): pl.pallas_call(functools.partial(gather_gate_kernel, n, pieces), in_specs...  177 us
    pallas_call x1, Pallas kernels, out_project(): pl.pallas_call(functools.partial(out_kernel, n), in_specs=[ANY, ANY, ANY,...  171 us
    pallas_call x1, Pallas kernels, gate_up(): pl.pallas_call(gate_kernel, grid=(rows // tile_rows, ff // tile), in_spec...  81.9 us
    pallas_call x2, Pallas kernels, project(): pl.pallas_call(functools.partial(proj_kernel, rope_heads, head), grid=(ro...  45.4 us
    pallas_call x1, Pallas kernels, attention(): pl.pallas_call(functools.partial(attn_kernel, group, head, tokens // 2),...  31.9 us
    all_gather x5, waiting for transfers between devices, gather(): return lax.all_gather(shard, GROUP_AXES, axis=axis, tiled=True)  22.7 us
    convert_element_type x1, other arithmetic, rms_norm(): return (hidden_f32 * lax.rsqrt(mean_sq + NORM_EPS) * gain).astype(BF16)  18.7 us
  transfers between devices with their start and end apart: 6, of which 1 were waited for; matrix products, arithmetic and copies ran while one was open for 5% of the time, Pallas kernels for 55%

commit v1 on v0

--- a/solution.py
+++ b/solution.py
@@ -129,7 +129,7 @@
     return lax.rem(me + (n - back if direction == 0 else back), n)
 
 
-def ring_matmul_scatter(n, me, sides, u_refs, w_ref, u_buf, w_buf, s_buf, r_buf, u_sem, w_sem, send_sem, recv_sem, finish):
+def ring_matmul_scatter(n, me, sides, u_refs, w_ref, u_buf, w_buf, s_buf, r_buf, u_sem, w_sem, send_sem, recv_sem, finish, hook=None):
     half = u_buf.shape[2]
     block = w_buf.shape[2]
     blocks = w_ref.shape[1] // block
@@ -187,6 +187,8 @@
                     send(step, d, cb).start()
                 else:
                     finish(d, cb, part)
+            if hook is not None:
+                hook(step, cb)
             return 0
 
         lax.fori_loop(0, blocks, one_block, 0)
@@ -272,6 +274,7 @@
     ff = u_ref.shape[1]
     tile = min(256, ff)
     tiles = ff // tile
+    turns = [(a, j) for a in range(n) for j in range(pieces)]
 
     def w_copies(t):
         out = []
@@ -283,12 +286,14 @@
     def rows_of(d, back, j):
         return pl.ds(pl.multiple_of(shard_of(me, d, back, n) * shard + d * half + j * piece, 16), piece)
 
+    def own_rows(d, j):
+        return b_ref.at[pl.ds(d * half + j * piece, piece), :]
+
     def hop(a, d, j):
         rows = rows_of(d, a, j)
-        src = b_ref.at[pl.ds(d * half + j * piece, piece), :] if a == 0 else all_ref.at[rows, :]
         return pltpu.make_async_remote_copy(
-            src_ref=src, dst_ref=all_ref.at[rows, :], send_sem=send_sem.at[a, d, j], recv_sem=recv_sem.at[a, d, j],
-            device_id={'tp': sides[d]}, device_id_type=MESH)
+            src_ref=own_rows(d, j) if a == 0 else all_ref.at[rows, :], dst_ref=all_ref.at[rows, :],
+            send_sem=send_sem.at[a, d, j], recv_sem=recv_sem.at[a, d, j], device_id={'tp': sides[d]}, device_id_type=MESH)
 
     def arrival(a, d, j):
         rows = rows_of(d, a + 1, j)
@@ -296,22 +301,34 @@
             src_ref=all_ref.at[rows, :], dst_ref=all_ref.at[rows, :], send_sem=send_sem.at[a, d, j], recv_sem=recv_sem.at[a, d, j],
             device_id={'tp': sides[d]}, device_id_type=MESH)
 
-    def x_copies(a):
+    def x_copies(k):
+        a, j = turns[k]
         return [pltpu.make_async_copy(
-            all_ref.at[pl.ds(pl.multiple_of(shard_of(me, d, a, n) * shard + d * half, 16), half), :],
-            x_buf.at[a % 2, pl.ds(d * half, half), :], x_sem.at[a % 2, d]) for d in range(2)]
-
-    def u_copies(a):
+            own_rows(d, j) if a == 0 else all_ref.at[rows_of(d, a, j), :],
+            x_buf.at[k % 2, pl.ds(d * piece, piece), :], x_sem.at[k % 2, d]) for d in range(2)]
+
+    def keep_copies(k):
+        a, j = turns[k]
         return [pltpu.make_async_copy(
-            u_buf.at[a % 2, pl.ds(d * half, half), :],
-            u_ref.at[pl.ds(pl.multiple_of(shard_of(me, d, a, n) * shard + d * half, 16), half), :], u_sem.at[a % 2, d]) for d in range(2)]
-
-    load_own = pltpu.make_async_copy(b_ref, x_buf.at[0], x_sem.at[0, 0])
-    load_own.start()
+            x_buf.at[k % 2, pl.ds(d * piece, piece), :], all_ref.at[rows_of(d, a, j), :], own_sem.at[j, d]) for d in range(2)]
+
+    def u_copies(k):
+        a, j = turns[k]
+        return [pltpu.make_async_copy(
+            u_buf.at[k % 2, pl.ds(d * piece, piece), :], u_ref.at[rows_of(d, a, j), :], u_sem.at[k % 2, d]) for d in range(2)]
+
+    def start(copies):
+        for c in copies:
+            c.start()
+
+    def wait(copies):
+        for c in copies:
+            c.wait()
+
+    start(x_copies(0))
 
     def load_w(t, _):
-        for c in w_copies(t):
-            c.start()
+        start(w_copies(t))
         return 0
 
     lax.fori_loop(0, tiles, load_w, 0)
@@ -319,40 +336,36 @@
     for j in range(pieces):
         for d in range(2):
             hop(0, d, j).start()
-    load_own.wait()
-    keep_own = pltpu.make_async_copy(x_buf.at[0], all_ref.at[pl.ds(pl.multiple_of(me * shard, 16), shard), :], own_sem)
-    keep_own.start()
-    for a in range(n):
+    for k, (a, j) in enumerate(turns):
         if a > 0:
-            for j in range(pieces):
-                for d in range(2):
-                    arrival(a - 1, d, j).wait_recv()
-                    if a + 1 < n:
-                        hop(a, d, j).start()
-            if a == 2:
-                keep_own.wait()
-            for c in x_copies(a):
-                c.start()
-            for c in x_copies(a):
-                c.wait()
-        if a >= 2:
-            for c in u_copies(a - 2):
-                c.wait()
-
-        def one_tile(t, _, a=a):
-            if a == 0:
-                for c in w_copies(t):
-                    c.wait()
+            for d in range(2):
+                arrival(a - 1, d, j).wait_recv()
+                if a + 1 < n:
+                    hop(a, d, j).start()
+            start(x_copies(k))
+        wait(x_copies(k))
+        if a == 0:
+            start(keep_copies(k))
+            if j > 0:
+                wait(keep_copies(k - 1))
+            if j + 1 < pieces:
+                start(x_copies(k + 1))
+        elif j == 0 and a == 1:
+            wait(keep_copies(k - 1))
+        if k >= 2:
+            wait(u_copies(k - 2))
+
+        def one_tile(t, _, k=k):
+            if k == 0:
+                wait(w_copies(t))
             at = pl.multiple_of(t * tile, tile)
-            u_buf[a % 2, :, pl.ds(at, tile)] = gated(x_buf[a % 2], w_buf[:, pl.ds(at, tile)], w_buf[:, pl.ds(ff + at, tile)])
+            u_buf[k % 2, :, pl.ds(at, tile)] = gated(x_buf[k % 2], w_buf[:, pl.ds(at, tile)], w_buf[:, pl.ds(ff + at, tile)])
             return 0
 
         lax.fori_loop(0, tiles, one_tile, 0)
-        for c in u_copies(a):
-            c.start()
-    for a in range(max(0, n - 2), n):
-        for c in u_copies(a):
-            c.wait()
+        start(u_copies(k))
+    for k in range(len(turns) - 2, len(turns)):
+        wait(u_copies(k))
     for a in range(n - 1):
         for j in range(pieces):
             for d in range(2):
@@ -364,6 +377,7 @@
     ff = w.shape[1] // 2
     tiles = ff // min(256, ff)
     pieces = 3
+    piece = shard // 2 // pieces
     rows = shard * n
     return pl.pallas_call(
         functools.partial(gather_gate_kernel, n, pieces),
@@ -372,11 +386,11 @@
         out_shape=[jax.ShapeDtypeStruct((rows, depth), BF16), jax.ShapeDtypeStruct((rows, ff), BF16)],
         scratch_shapes=[
             pltpu.VMEM((depth, 2 * ff), BF16),
-            pltpu.VMEM((2, shard, depth), BF16),
-            pltpu.VMEM((2, shard, ff), BF16),
+            pltpu.VMEM((2, 2 * piece, depth), BF16),
+            pltpu.VMEM((2, 2 * piece, ff), BF16),
             pltpu.SemaphoreType.DMA((tiles, 2)),
             pltpu.SemaphoreType.DMA((2, 2)),
-            pltpu.SemaphoreType.DMA,
+            pltpu.SemaphoreType.DMA((pieces, 2)),
             pltpu.SemaphoreType.DMA((2, 2)),
             pltpu.SemaphoreType.DMA((n - 1, 2, pieces)),
             pltpu.SemaphoreType.DMA((n - 1, 2, pieces)),
@@ -409,83 +423,146 @@
     )(x, w, w)
 
 
-def down_kernel(n, ua_ref, ub_ref, w_ref, r_ref, y_ref, res_buf, res_sem, own_sem, ag_send, ag_recv,
+def part_cols(part, block, cb):
+    return pl.ds(pl.multiple_of((2 * cb + part) * block, block), block)
+
+
+def load_resid(r_ref, res_buf, res_sem, part, block, blocks):
+    def copy(cb):
+        return pltpu.make_async_copy(r_ref.at[:, part_cols(part, block, cb)], res_buf.at[cb], res_sem.at[cb])
+
+    def begin(cb, _):
+        copy(cb).start()
+        return 0
+
+    def end(cb, _):
+        copy(cb).wait()
+        return 0
+
+    return lambda: lax.fori_loop(0, blocks, begin, 0), lambda: lax.fori_loop(0, blocks, end, 0)
+
+
+def down_sum_kernel(n, ua_ref, ub_ref, w_ref, r_ref, y_ref, res_buf, res_sem, u_buf, w_buf, s_buf, r_buf, u_sem, w_sem, send_sem, recv_sem):
+    me, right, left = ring_place(n)
+    half = r_ref.shape[0] // 2
+    blocks, _, block = res_buf.shape
+    begin, end = load_resid(r_ref, res_buf, res_sem, 0, block, blocks)
+    begin()
+    ring_barrier(right, left)
+    end()
+
+    def finish(d, cb, part):
+        total = res_buf[cb, pl.ds(d * half, half), :].astype(F32) + part.astype(BF16).astype(F32)
+        y_ref[d, cb] = total.astype(BF16)
+
+    ring_matmul_scatter(n, me, (right, left), [ua_ref, ub_ref], w_ref, u_buf, w_buf, s_buf, r_buf, u_sem, w_sem, send_sem, recv_sem, finish)
+
+
+def down_kernel(n, ua_ref, ub_ref, w_ref, r_ref, first_ref, y_ref, res_buf, res_sem, own_sem, ag_send, ag_recv,
                 u_buf, w_buf, s_buf, r_buf, u_sem, w_sem, send_sem, recv_sem):
     me, right, left = ring_place(n)
     sides = (right, left)
     shard = r_ref.shape[0]
     half = shard // 2
-    block = w_buf.shape[2]
-    blocks = w_ref.shape[1] // block
-    load_r = pltpu.make_async_copy(r_ref, res_buf, res_sem)
-    load_r.start()
+    blocks, _, block = res_buf.shape
+    begin, end = load_resid(r_ref, res_buf, res_sem, 1, block, blocks)
+    begin()
     ring_barrier(right, left)
-    load_r.wait()
-
-    def place(d, back, cb):
+
+    def place(d, back, part, cb):
         row = pl.multiple_of(shard_of(me, d, back, n) * shard + d * half, 16)
-        return y_ref.at[pl.ds(row, half), pl.ds(pl.multiple_of(cb * block, block), block)]
-
-    def hop(a, d, cb):
-        src = r_buf.at[n - 2, d, cb] if a == 0 else place(d, a, cb)
+        return y_ref.at[pl.ds(row, half), part_cols(part, block, cb)]
+
+    def own(d, part, cb):
+        return first_ref.at[d, cb] if part == 0 else r_buf.at[n - 2, d, cb]
+
+    def hop(a, d, part, cb):
         return pltpu.make_async_remote_copy(
-            src_ref=src, dst_ref=place(d, a, cb), send_sem=ag_send.at[a, d, cb], recv_sem=ag_recv.at[a, d, cb],
-            device_id={'tp': sides[d]}, device_id_type=MESH)
-
-    def arrival(a, d, cb):
+            src_ref=own(d, part, cb) if a == 0 else place(d, a, part, cb), dst_ref=place(d, a, part, cb),
+            send_sem=ag_send.at[a, d, part, cb], recv_sem=ag_recv.at[a, d, part, cb], device_id={'tp': sides[d]}, device_id_type=MESH)
+
+    def arrival(a, d, part, cb):
         return pltpu.make_async_remote_copy(
-            src_ref=place(d, a + 1, cb), dst_ref=place(d, a + 1, cb), send_sem=ag_send.at[a, d, cb], recv_sem=ag_recv.at[a, d, cb],
-            device_id={'tp': sides[d]}, device_id_type=MESH)
-
-    def keep(d, cb):
-        return pltpu.make_async_copy(r_buf.at[n - 2, d, cb], place(d, 0, cb), own_sem.at[d, cb])
+            src_ref=place(d, a + 1, part, cb), dst_ref=place(d, a + 1, part, cb),
+            send_sem=ag_send.at[a, d, part, cb], recv_sem=ag_recv.at[a, d, part, cb], device_id={'tp': sides[d]}, device_id_type=MESH)
+
+    def keep(d, part, cb):
+        return pltpu.make_async_copy(own(d, part, cb), place(d, 0, part, cb), own_sem.at[d, part, cb])
+
+    def forward(a, part, cb):
+        for d in range(2):
+            arrival(a, d, part, cb).wait_recv()
+            if a + 1 < n - 1:
+                hop(a + 1, d, part, cb).start()
+
+    def send_first(cb, _):
+        for d in range(2):
+            hop(0, d, 0, cb).start()
+            keep(d, 0, cb).start()
+        return 0
+
+    lax.fori_loop(0, blocks, send_first, 0)
+    end()
 
     def finish(d, cb, part):
-        rows, cols = pl.ds(d * half, half), pl.ds(pl.multiple_of(cb * block, block), block)
-        total = res_buf[rows, cols].astype(F32) + part.astype(BF16).astype(F32)
+        total = res_buf[cb, pl.ds(d * half, half), :].astype(F32) + part.astype(BF16).astype(F32)
         r_buf[n - 2, d, cb] = total.astype(BF16)
-        hop(0, d, cb).start()
-        keep(d, cb).start()
-
-    ring_matmul_scatter(n, me, sides, [ua_ref, ub_ref], w_ref, u_buf, w_buf, s_buf, r_buf, u_sem, w_sem, send_sem, recv_sem, finish)
+        hop(0, d, 1, cb).start()
+        keep(d, 1, cb).start()
+
+    def hook(step, cb):
+        if step > 0:
+            forward(step - 1, 0, cb)
+
+    ring_matmul_scatter(n, me, sides, [ua_ref, ub_ref], w_ref, u_buf, w_buf, s_buf, r_buf, u_sem, w_sem, send_sem, recv_sem, finish, hook)
     for a in range(n - 1):
-        def forward(cb, _, a=a):
+        def last(cb, _, a=a):
+            forward(a, 1, cb)
+            return 0
+
+        lax.fori_loop(0, blocks, last, 0)
+
+    def drain(cb, _):
+        for part in range(2):
             for d in range(2):
-                arrival(a, d, cb).wait_recv()
-                if a + 1 < n - 1:
-                    hop(a + 1, d, cb).start()
-            return 0
-
-        lax.fori_loop(0, blocks, forward, 0)
-
-    def drain(cb, _):
-        for d in range(2):
-            keep(d, cb).wait()
-            for a in range(n - 1):
-                hop(a, d, cb).wait_send()
+                keep(d, part, cb).wait()
+                for a in range(n - 1):
+                    hop(a, d, part, cb).wait_send()
         return 0
 
     lax.fori_loop(0, blocks, drain, 0)
 
 
-def down_project(n, act_a, act_b, w_down, resid):
+def down_project(n, act_a, act_b, w_first, w_second, resid, blocks):
     rows = act_a.shape[0]
-    depth, width = w_down.shape
+    depth, part = w_first.shape
     shard = rows // n
-    block = min(512, width // 2)
-    blocks = width // block
+    block = part // blocks
+    half = shard // 2
+    resid_scratch = [pltpu.VMEM((blocks, shard, block), BF16), pltpu.SemaphoreType.DMA((blocks,))]
+    ring = ring_scratch(n, half, depth, block, blocks, 2)
+    params = dict(has_side_effects=True, vmem_limit_bytes=VMEM_LIMIT)
+    first = pl.pallas_call(
+        functools.partial(down_sum_kernel, n),
+        in_specs=[ANY] * 4,
+        out_specs=VMEM,
+        out_shape=jax.ShapeDtypeStruct((2, blocks, half, block), BF16),
+        scratch_shapes=resid_scratch + ring,
+        compiler_params=pltpu.CompilerParams(collective_id=2, **params),
+        cost_estimate=cost(2 * rows * depth * part * 2, 2 * (rows * depth + depth * part)),
+    )(act_a, act_b, w_first, resid)
     return pl.pallas_call(
         functools.partial(down_kernel, n),
-        in_specs=[ANY, ANY, ANY, ANY],
+        in_specs=[ANY] * 5,
         out_specs=ANY,
-        out_shape=jax.ShapeDtypeStruct((rows, width), BF16),
-        scratch_shapes=[
-            pltpu.VMEM((shard, width), BF16), pltpu.SemaphoreType.DMA, pltpu.SemaphoreType.DMA((2, blocks)),
-            pltpu.SemaphoreType.DMA((n - 1, 2, blocks)), pltpu.SemaphoreType.DMA((n - 1, 2, blocks)),
-        ] + ring_scratch(n, shard // 2, depth, block, blocks, 2),
-        compiler_params=pltpu.CompilerParams(collective_id=2, has_side_effects=True, vmem_limit_bytes=VMEM_LIMIT),
-        cost_estimate=cost(2 * rows * depth * width * 4, 2 * (rows * depth + depth * width)),
-    )(act_a, act_b, w_down, resid)
+        out_shape=jax.ShapeDtypeStruct((rows, 2 * part), BF16),
+        scratch_shapes=resid_scratch + [
+            pltpu.SemaphoreType.DMA((2, 2, blocks)),
+            pltpu.SemaphoreType.DMA((n - 1, 2, 2, blocks)), pltpu.SemaphoreType.DMA((n - 1, 2, 2, blocks)),
+        ] + ring,
+        compiler_params=pltpu.CompilerParams(collective_id=3, **params),
+        cost_estimate=cost(2 * rows * depth * part * 6, 2 * (rows * depth + depth * part)),
+    )(act_a, act_b, w_second, resid, first)
 
 
 def gather(shard, axis):
@@ -509,15 +586,17 @@
         kv_heads = w_key.shape[1]
         rows = n_seqs * tokens
         local = w_query.shape[0]
-        ff_half = w_gate.shape[1] // 2
+        ff_a = w_gate.shape[1] * 9 // 14 // 256 * 256
         x = hidden.reshape(rows, d_model)
 
         w_qkv = jnp.concatenate([w.reshape(local, -1) for w in (w_query, w_key, w_value)], axis=1)
         full_qkv = gather(w_qkv, 0)
         full_out = gather(w_out.reshape(heads * head, -1), 1)
-        full_a = gather(jnp.concatenate([w_gate[:, :ff_half], w_up[:, :ff_half]], axis=1), 0)
-        full_b = gather(jnp.concatenate([w_gate[:, ff_half:], w_up[:, ff_half:]], axis=1), 0)
-        full_down = gather(w_down, 1)
+        full_a = gather(jnp.concatenate([w_gate[:, :ff_a], w_up[:, :ff_a]], axis=1), 0)
+        full_b = gather(jnp.concatenate([w_gate[:, ff_a:], w_up[:, ff_a:]], axis=1), 0)
+        down_half = w_down.shape[1] // 2
+        full_down0 = gather(w_down[:, :down_half], 1)
+        full_down1 = gather(w_down[:, down_half:], 1)
 
         normed = rms_norm(x.astype(F32), attn_gain)
         inv_freq = ROPE_THETA ** (-jnp.arange(0, head, 2, dtype=F32) / head)
@@ -534,7 +613,7 @@
         resid, normed_mlp = out_project(n_tp, mixed, full_out, x, mlp_gain.reshape(1, d_model))
         all_normed, act_a = gather_gate(n_tp, normed_mlp, full_a)
         act_b = gate_up(all_normed, full_b, rows // n_tp)
-        y = down_project(n_tp, act_a, act_b, full_down, resid)
+        y = down_project(n_tp, act_a, act_b, full_down0, full_down1, resid, full_down0.shape[1] // down_half)
         return y.reshape(hidden.shape)
 
     return jax.shard_map(

time: 934 us -> 913 us (0.978)
  Pallas kernels: 820 us -> 798 us
    pallas_call x1, Pallas kernels: 81.9 us -> 63.1 us  [gate_up(): pl.pallas_call(gate_kernel, grid=(rows // tile_rows, ff // tile), in_spec...]
    pallas_call x1, Pallas kernels: 177 us -> 166 us  [gather_gate(): pl.pallas_call(functools.partial(gather_gate_kernel, n, pieces), in_specs...]
    pallas_call x1 -> x2, Pallas kernels: 313 us -> 321 us  [the longest x1 232 us: down_project(): pl.pallas_call(functools.partial(down_kernel, n), in_specs=[ANY] * 5, out...]
    all_gather x5 -> x6, waiting for transfers between devices: 22.7 us -> 21.4 us  [gather(): return lax.all_gather(shard, GROUP_AXES, axis=axis, tiled=True)]
  transfers between devices with their start and end apart: 6 -> 7, of which waited for: 1 -> 1; matrix products, arithmetic and copies ran while one was open for 5% -> 5% of each run, Pallas kernels for 55% -> 63%
where the time goes in v1:
time: 913 us; the launch traced here: 902 us
  Pallas kernels  798 us (87%)
  other arithmetic  39.2 us (4%)
  local copies, waits for them, and re-layouts  27.9 us (3%)
  waiting for transfers between devices  22.4 us (2%)
  between operations  13.8 us (2%)
    pallas_call x1, Pallas kernels, down_project(): pl.pallas_call(functools.partial(down_kernel, n), in_specs=[ANY] * 5, out...  232 us
    pallas_call x1, Pallas kernels, out_project(): pl.pallas_call(functools.partial(out_kernel, n), in_specs=[ANY, ANY, ANY,...  171 us
    pallas_call x1, Pallas kernels, gather_gate(): pl.pallas_call(functools.partial(gather_gate_kernel, n, pieces), in_specs...  166 us
    pallas_call x1, Pallas kernels, down_project(): pl.pallas_call(functools.partial(down_sum_kernel, n), in_specs=[ANY] * 4,...  88.3 us
    pallas_call x1, Pallas kernels, gate_up(): pl.pallas_call(gate_kernel, grid=(rows // tile_rows, ff // tile), in_spec...  63.1 us
    pallas_call x2, Pallas kernels, project(): pl.pallas_call(functools.partial(proj_kernel, rope_heads, head), grid=(ro...  45.4 us
    pallas_call x1, Pallas kernels, attention(): pl.pallas_call(functools.partial(attn_kernel, group, head, tokens // 2),...  31.6 us
    all_gather x6, waiting for transfers between devices, gather(): return lax.all_gather(shard, GROUP_AXES, axis=axis, tiled=True)  21.4 us
  transfers between devices with their start and end apart: 7, of which 1 were waited for; matrix products, arithmetic and copies ran while one was open for 5% of the time, Pallas kernels for 63%

profile of v1, /device:TPU:97, one launch (start us, length us, event | category | flops | bytes accessed | tf_op | source)
XLA Modules:
  0.0 902.1 jit_solution(18022450325392184796)
XLA Ops:
  6.5 0.0 all-gather.7.cloned.1.call-start
  6.6 1.5 copy.18
  8.0 1.1 copy_bitcast_fusion.1
  9.2 1.3 pad_maximum_fusion.2
  10.4 0.1 all-gather.7.cloned.1.call-update
  10.5 0.1 all-gather.9.cloned.1.call-start
  10.5 0.7 all-gather.9.cloned.1.call-update
  11.3 0.1 all-gather.11.cloned.1.call-start
  11.4 0.0 slice-start
  11.4 0.0 slice-start.2
  11.4 1.6 slice-done
  13.0 0.7 slice-done.2
  13.7 2.5 pad_maximum_fusion
  16.2 0.1 all-gather.11.cloned.1.call-update
  16.3 0.0 slice-start.1
  16.3 0.0 slice-start.3
  16.3 0.1 all-gather.13.cloned.1.call-start
  16.4 1.2 slice-done.1
  17.6 0.4 slice-done.3
  18.0 1.7 pad_maximum_fusion.1
  19.7 0.1 all-gather.13.cloned.1.call-update
  19.8 0.0 copy-start.1
  19.8 0.1 all-gather.17.cloned.1.call-start
  19.8 4.5 fusion.1
  24.4 0.1 all-gather.17.cloned.1.call-update
  24.4 0.1 all-gather.15.cloned.1.call-start
  24.5 0.0 copy-done.1
  24.5 8.6 multiply_reduce_fusion
  33.2 4.2 fusion
  37.4 0.0 copy-start
  37.4 2.1 pad_maximum_fusion.3
  39.5 0.0 copy-done
  39.5 18.9 %multiply_convert_fusion.x_ref = bf16[2304,4096]{1,0:T(8,128)(2,1)} fusion(f32[4096]{0:T(1024)S(1)} %copy-done, f32[2304]{0:T(1024)S(1)} %rsqrt.12, bf16[3,768,4096]{2,1,0:T(8,128)(2,1)} %param.11), kind=kLoop, calls=%fused_computation | loop fusion | flops 37748736 | bytes 37774336 | tf_op jit(solution)/shard_map/convert_element_type | solution.py:25
  58.4 21.3 %all-gather.7.cloned.1.call-done.w_ref = bf16[4096,1536]{1,0:T(8,128)(2,1)} async-done(((bf16[512,1536]{1,0:T(8,128)(2,1)}), bf16[4096,1536]{1,0:T(8,128)(2,1)}) %all-gather.7.cloned.1.call-update) | async-done | bytes 12582928 | tf_op jit(solution)/shard_map/all_gather | solution.py:569
  79.7 17.8 %shard_map.110.ko_ref.vo_ref = bf16[2304,512]{1,0:T(8,128)(2,1)} custom-call(bf16[2304,4096]{1,0:T(8,128)(2,1)} %multiply_convert_fusion.x_ref, bf16[4096,1536]{1,0:T(8,128)(2,1)} %all-gather.7.cloned.1.call-done.w_ref, f32[2304,128]{1,0:T(8,128)} %get-tuple-element.20.cos_ref, f32[2304,128]{1,0:T(8,128)} %get-tuple-element.21.sin_ref), custom_call_target="tpu_custom_call" | custom-call | flops 9663676416 | bytes 25427968 | tf_op jit(solution)/shard_map/pallas_call | solution.py:45
  97.4 0.3 collective-permute-start
  97.7 0.1 all-gather.15.cloned.1.call-update
  97.7 27.6 %shard_map.109.q_ref = bf16[2304,1024]{1,0:T(8,128)(2,1)} custom-call(bf16[2304,4096]{1,0:T(8,128)(2,1)} %multiply_convert_fusion.x_ref, bf16[4096,1536]{1,0:T(8,128)(2,1)} %all-gather.7.cloned.1.call-done.w_ref, f32[2304,128]{1,0:T(8,128)} %get-tuple-element.20.cos_ref, f32[2304,128]{1,0:T(8,128)} %get-tuple-element.21.sin_ref), custom_call_target="tpu_custom_call" | custom-call | flops 19327352832 | bytes 31981568 | tf_op jit(solution)/shard_map/pallas_call | solution.py:45
  125.4 0.0 collective-permute-done.kp_ref.vp_ref
  125.4 31.6 %shard_map.111.o_ref = bf16[2304,1024]{1,0:T(8,128)(2,1)} custom-call(bf16[2304,1024]{1,0:T(8,128)(2,1)} %shard_map.109.q_ref, bf16[2304,512]{1,0:T(8,128)(2,1)} %shard_map.110.ko_ref.vo_ref, bf16[2304,512]{1,0:T(8,128)(2,1)} %shard_map.110.ko_ref.vo_ref, bf16[2304,512]{1,0:T(8,128)(2,1)} %collective-permute-done.kp_ref.vp_ref, ...), custom_call_target="tpu_custom_call" | custom-call | flops 18119393280 | bytes 9437184 | tf_op jit(solution)/shard_map/pallas_call | solution.py:105
  157.0 0.0 all-gather.9.cloned.1.call-done.w_ref
  157.0 171.2 %shard_map.112 = (bf16[576,4096]{1,0:T(8,128)(2,1)}, bf16[576,4096]{1,0:T(8,128)(2,1)}) custom-call(bf16[2304,1024]{1,0:T(8,128)(2,1)} %shard_map.111.o_ref, bf16[1024,4096]{1,0:T(8,128)(2,1)} %all-gather.9.cloned.1.call-done.w_ref, bf16[2304,4096]{1,0:T(8,128)(2,1)} %bitcast.15, f32[1,4096]{1,0:T(1,128)} %bitcast.22), custom_call_target="tpu_custom_call" | custom-call | flops 96636764160 | bytes 13107200 | tf_op jit(solution)/shard_map/pallas_call | solution.py:250
  328.2 0.0 all-gather.11.cloned.1.call-done.w_ref
  328.3 166.2 %shard_map.113 = (bf16[2304,4096]{1,0:T(8,128)(2,1)}, bf16[2304,2304]{1,0:T(8,128)(2,1)}) custom-call(bf16[576,4096]{1,0:T(8,128)(2,1)} %get-tuple-element.9.b_ref, bf16[4096,4608]{1,0:T(8,128)(2,1)} %all-gather.11.cloned.1.call-done.w_ref), custom_call_target="tpu_custom_call" | custom-call | flops 173946175488 | bytes 56623104 | tf_op jit(solution)/shard_map/pallas_call | solution.py:382
  494.4 0.0 all-gather.13.cloned.1.call-done.g_ref.u_ref
  494.5 63.1 %shard_map.114.ub_ref = bf16[2304,1280]{1,0:T(8,128)(2,1)} custom-call(bf16[2304,4096]{1,0:T(8,128)(2,1)} %get-tuple-element.11.x_ref, bf16[4096,2560]{1,0:T(8,128)(2,1)} %all-gather.13.cloned.1.call-done.g_ref.u_ref, bf16[4096,2560]{1,0:T(8,128)(2,1)} %all-gather.13.cloned.1.call-done.g_ref.u_ref), custom_call_target="tpu_custom_call" | custom-call | flops 48318382080 | bytes 39845888 | tf_op jit(solution)/shard_map/pallas_call | solution.py:411
  557.6 0.0 all-gather.17.cloned.1.call-done.w_ref
  557.6 88.3 %shard_map.115.first_ref = bf16[2,8,288,256]{3,2,1,0:T(8,128)(2,1)} custom-call(bf16[2304,2304]{1,0:T(8,128)(2,1)} %get-tuple-element.10.ua_ref, bf16[2304,1280]{1,0:T(8,128)(2,1)} %shard_map.114.ub_ref, bf16[3584,2048]{1,0:T(8,128)(2,1)} %all-gather.17.cloned.1.call-done.w_ref, bf16[576,4096]{1,0:T(8,128)(2,1)} %get-tuple-element.12.r_ref), custom_call_target="tpu_custom_call" | custom-call | flops 67645734912 | bytes 31195136 | tf_op jit(solution)/shard_map/pallas_call | solution.py:545
  645.9 0.0 all-gather.15.cloned.1.call-done.w_ref
  645.9 232.4 %shard_map.116 = bf16[2304,4096]{1,0:T(8,128)(2,1)} custom-call(bf16[2304,2304]{1,0:T(8,128)(2,1)} %get-tuple-element.10.ua_ref, bf16[2304,1280]{1,0:T(8,128)(2,1)} %shard_map.114.ub_ref, bf16[3584,2048]{1,0:T(8,128)(2,1)} %all-gather.15.cloned.1.call-done.w_ref, bf16[576,4096]{1,0:T(8,128)(2,1)} %get-tuple-element.12.r_ref, ...), custom_call_target="tpu_custom_call" | custom-call | flops 202937204736 | bytes 31195136 | tf_op jit(solution)/shard_map/pallas_call | solution.py:554
  878.3 16.8 %copy.20 = bf16[3,768,4096]{2,1,0:T(8,128)(2,1)} copy(bf16[3,768,4096]{2,1,0:T(8,128)(2,1)} %bitcast.16) | data formatting | bytes 37748736
  (5 shorter events, 0.1 us)
Async XLA Ops:
  6.5 73.1 %all-gather.7.cloned.1.call-start = ((), (), s32[]{:S(2)}) async-start(), calls=%async_computation | async-start | bytes 14155776 | tf_op jit(solution)/shard_map/all_gather | solution.py:569
  10.5 146.5 %all-gather.9.cloned.1.call-start = ((), (), s32[]{:S(2)}) async-start(), calls=%async_computation.1 | async-start | bytes 9437184 | tf_op jit(solution)/shard_map/all_gather | solution.py:569
  11.3 317.0 %all-gather.11.cloned.1.call-start = ((), (), s32[]{:S(2)}) async-start(), calls=%async_computation.2 | async-start | bytes 42467328 | tf_op jit(solution)/shard_map/all_gather | solution.py:569
  11.4 1.7 slice-start
  11.4 2.4 slice-start.2
  16.3 1.3 slice-start.1
  16.3 1.7 slice-start.3
  16.3 478.1 %all-gather.13.cloned.1.call-start = ((), (), s32[]{:S(2)}) async-start(), calls=%async_computation.3 | async-start | bytes 23592960 | tf_op jit(solution)/shard_map/all_gather | solution.py:569
  19.8 4.7 copy-start.1
  19.8 537.8 %all-gather.17.cloned.1.call-start = ((), (), s32[]{:S(2)}) async-start(), calls=%async_computation.5 | async-start | bytes 16515072 | tf_op jit(solution)/shard_map/all_gather | solution.py:569
  24.4 621.4 %all-gather.15.cloned.1.call-start = ((), (), s32[]{:S(2)}) async-start(), calls=%async_computation.4 | async-start | bytes 16515072 | tf_op jit(solution)/shard_map/all_gather | solution.py:569
  37.4 2.1 copy-start
  97.4 28.0 %collective-permute-start = (bf16[2304,512]{1,0:T(8,128)(2,1)}, bf16[2304,512]{1,0:T(8,128)(2,1)}, u32[]{:S(2)}, u32[]{:S(2)}) collective-permute-start(bf16[2304,512]{1,0:T(8,128)(2,1)} %shard_map.110.ko_ref.vo_ref), channel_id=1, source_target_pairs={{0,1},{1,0},{2,3},{3,2},{4,5},{5,4},{6,7},{7,6},{8,9},{9,8},{10,11... | collective-permute-start | bytes 7077896 | tf_op jit(solution)/shard_map/ppermute | solution.py:610
Sparse Core Ops, SparseCore 0:
  10.6 69.0 all-gather.6
  81.3 47.4 all-gather.8
  130.4 172.8 all-gather.10
  304.8 99.0 all-gather.12
  405.3 78.9 all-gather.16
  485.8 79.0 all-gather.14

commit v2 on v1

--- a/solution.py
+++ b/solution.py
@@ -129,7 +129,7 @@
     return lax.rem(me + (n - back if direction == 0 else back), n)
 
 
-def ring_matmul_scatter(n, me, sides, u_refs, w_ref, u_buf, w_buf, s_buf, r_buf, u_sem, w_sem, send_sem, recv_sem, finish, hook=None):
+def ring_matmul_scatter(n, me, sides, u_refs, w_ref, u_buf, w_buf, s_buf, r_buf, u_sem, w_sem, send_sem, recv_sem, finish, hook=None, prepare=None):
     half = u_buf.shape[2]
     block = w_buf.shape[2]
     blocks = w_ref.shape[1] // block
@@ -163,6 +163,8 @@
         if step + 1 < n:
             for c in u_copies(step + 1):
                 c.start()
+        if prepare is not None:
+            prepare(step)
 
         def one_block(cb, _, step=step):
             slot = lax.rem(cb, 2)
@@ -223,14 +225,17 @@
     load_h = pltpu.make_async_copy(h_ref.at[pl.ds(pl.multiple_of(me * shard, 16), shard), :], h_buf, h_sem)
     load_h.start()
     ring_barrier(right, left)
-    load_h.wait()
+
+    def prepare(step):
+        if step == n - 1:
+            load_h.wait()
 
     def finish(d, cb, part):
         rows, cols = pl.ds(d * half, half), pl.ds(pl.multiple_of(cb * block, block), block)
         total = h_buf[rows, cols].astype(F32) + part.astype(BF16).astype(F32)
         r_ref[rows, cols] = total.astype(BF16)
 
-    ring_matmul_scatter(n, me, (right, left), [o_ref], w_ref, u_buf, w_buf, s_buf, r_buf, u_sem, w_sem, send_sem, recv_sem, finish)
+    ring_matmul_scatter(n, me, (right, left), [o_ref], w_ref, u_buf, w_buf, s_buf, r_buf, u_sem, w_sem, send_sem, recv_sem, finish, prepare=prepare)
     gain = gain_ref[...]
 
     def norm_rows(i, _):
@@ -400,27 +405,15 @@
     )(b, w)
 
 
-def gate_kernel(x_ref, g_ref, u_ref, o_ref):
-    o_ref[...] = gated(x_ref[...], g_ref[...], u_ref[...])
-
-
-def gate_up(x, w, tile_rows):
-    rows, depth = x.shape
-    ff = w.shape[1] // 2
-    tile = min(256, ff)
+def copy_kernel(x_ref, o_ref):
+    o_ref[...] = x_ref[...]
+
+
+def plain_copy(x, tile):
+    spec = pl.BlockSpec((tile, x.shape[1]), lambda i: (i, 0))
     return pl.pallas_call(
-        gate_kernel,
-        grid=(rows // tile_rows, ff // tile),
-        in_specs=[
-            pl.BlockSpec((tile_rows, depth), lambda i, j: (i, 0)),
-            pl.BlockSpec((depth, tile), lambda i, j: (0, j)),
-            pl.BlockSpec((depth, tile), lambda i, j: (0, ff // tile + j)),
-        ],
-        out_specs=pl.BlockSpec((tile_rows, tile), lambda i, j: (i, j)),
-        out_shape=jax.ShapeDtypeStruct((rows, ff), BF16),
-        compiler_params=pltpu.CompilerParams(vmem_limit_bytes=VMEM_LIMIT),
-        cost_estimate=cost(4 * rows * depth * ff, 2 * rows * depth + 2 * w.size),
-    )(x, w, w)
+        copy_kernel, grid=(x.shape[0] // tile,), in_specs=[spec], out_specs=spec, out_shape=jax.ShapeDtypeStruct(x.shape, x.dtype),
+        cost_estimate=cost(1000, 4 * x.size))(x)
 
 
 def part_cols(part, block, cb):
@@ -442,20 +435,81 @@
     return lambda: lax.fori_loop(0, blocks, begin, 0), lambda: lax.fori_loop(0, blocks, end, 0)
 
 
-def down_sum_kernel(n, ua_ref, ub_ref, w_ref, r_ref, y_ref, res_buf, res_sem, u_buf, w_buf, s_buf, r_buf, u_sem, w_sem, send_sem, recv_sem):
+def down_sum_kernel(n, x_ref, wb_ref, ua_ref, w_ref, r_ref, y_ref, ub_ref, wb_buf, x_buf, wb_sem, x_sem, ub_sem, res_buf, res_sem,
+                    u_buf, w_buf, s_buf, r_buf, u_sem, w_sem, send_sem, recv_sem):
     me, right, left = ring_place(n)
     half = r_ref.shape[0] // 2
     blocks, _, block = res_buf.shape
+    ff_a, ff = ua_ref.shape[1], ub_ref.shape[1]
+    tile = min(256, ff)
+    tiles = ff // tile
     begin, end = load_resid(r_ref, res_buf, res_sem, 0, block, blocks)
+
+    def rows_of(d, step):
+        return pl.ds(pl.multiple_of(shard_of(me, d, step + 1, n) * (2 * half) + d * half, 16), half)
+
+    def x_copies(step):
+        return [pltpu.make_async_copy(x_ref.at[rows_of(d, step), :], x_buf.at[pl.ds(d * half, half), :], x_sem.at[d]) for d in range(2)]
+
+    def wb_copies(t):
+        out = []
+        for i in range(2):
+            cols = pl.ds(pl.multiple_of(i * ff + t * tile, tile), tile)
+            out.append(pltpu.make_async_copy(wb_ref.at[:, cols], wb_buf.at[:, cols], wb_sem.at[t, i]))
+        return out
+
+    def ub_copies(step):
+        return [pltpu.make_async_copy(
+            u_buf.at[step % 2, d, :, pl.ds(ff_a, ff)], ub_ref.at[rows_of(d, step), :], ub_sem.at[step % 2, d]) for d in range(2)]
+
+    for c in x_copies(0):
+        c.start()
+
+    def load_wb(t, _):
+        for c in wb_copies(t):
+            c.start()
+        return 0
+
+    lax.fori_loop(0, tiles, load_wb, 0)
     begin()
     ring_barrier(right, left)
-    end()
+
+    def prepare(step):
+        for c in x_copies(step):
+            c.wait()
+        if step >= 2:
+            for c in ub_copies(step - 2):
+                c.wait()
+
+        def one_tile(t, _):
+            if step == 0:
+                for c in wb_copies(t):
+                    c.wait()
+            at = pl.multiple_of(t * tile, tile)
+            act = gated(x_buf[...], wb_buf[:, pl.ds(at, tile)], wb_buf[:, pl.ds(ff + at, tile)])
+            to = pl.ds(pl.multiple_of(ff_a + t * tile, tile), tile)
+            for d in range(2):
+                u_buf[step % 2, d, :, to] = act[d * half:(d + 1) * half, :]
+            return 0
+
+        lax.fori_loop(0, tiles, one_tile, 0)
+        for c in ub_copies(step):
+            c.start()
+        if step + 1 < n:
+            for c in x_copies(step + 1):
+                c.start()
+        else:
+            end()
 
     def finish(d, cb, part):
         total = res_buf[cb, pl.ds(d * half, half), :].astype(F32) + part.astype(BF16).astype(F32)
         y_ref[d, cb] = total.astype(BF16)
 
-    ring_matmul_scatter(n, me, (right, left), [ua_ref, ub_ref], w_ref, u_buf, w_buf, s_buf, r_buf, u_sem, w_sem, send_sem, recv_sem, finish)
+    ring_matmul_scatter(n, me, (right, left), [ua_ref], w_ref, u_buf, w_buf, s_buf, r_buf, u_sem, w_sem, send_sem, recv_sem, finish,
+                        prepare=prepare)
+    for step in range(max(0, n - 2), n):
+        for c in ub_copies(step):
+            c.wait()
 
 
 def down_kernel(n, ua_ref, ub_ref, w_ref, r_ref, first_ref, y_ref, res_buf, res_sem, own_sem, ag_send, ag_recv,
@@ -502,7 +556,10 @@
         return 0
 
     lax.fori_loop(0, blocks, send_first, 0)
-    end()
+
+    def prepare(step):
+        if step == n - 1:
+            end()
 
     def finish(d, cb, part):
         total = res_buf[cb, pl.ds(d * half, half), :].astype(F32) + part.astype(BF16).astype(F32)
@@ -514,7 +571,8 @@
         if step > 0:
             forward(step - 1, 0, cb)
 
-    ring_matmul_scatter(n, me, sides, [ua_ref, ub_ref], w_ref, u_buf, w_buf, s_buf, r_buf, u_sem, w_sem, send_sem, recv_sem, finish, hook)
+    ring_matmul_scatter(n, me, sides, [ua_ref, ub_ref], w_ref, u_buf, w_buf, s_buf, r_buf, u_sem, w_sem, send_sem, recv_sem, finish,
+                        hook=hook, prepare=prepare)
     for a in range(n - 1):
         def last(cb, _, a=a):
             forward(a, 1, cb)
@@ -533,24 +591,29 @@
     lax.fori_loop(0, blocks, drain, 0)
 
 
-def down_project(n, act_a, act_b, w_first, w_second, resid, blocks):
-    rows = act_a.shape[0]
+def down_project(n, normed, w_b, act_a, w_first, w_second, resid, blocks):
+    rows, width = normed.shape
     depth, part = w_first.shape
+    ff = w_b.shape[1] // 2
+    tiles = ff // min(256, ff)
     shard = rows // n
     block = part // blocks
     half = shard // 2
     resid_scratch = [pltpu.VMEM((blocks, shard, block), BF16), pltpu.SemaphoreType.DMA((blocks,))]
-    ring = ring_scratch(n, half, depth, block, blocks, 2)
     params = dict(has_side_effects=True, vmem_limit_bytes=VMEM_LIMIT)
-    first = pl.pallas_call(
+    first, act_b = pl.pallas_call(
         functools.partial(down_sum_kernel, n),
-        in_specs=[ANY] * 4,
-        out_specs=VMEM,
-        out_shape=jax.ShapeDtypeStruct((2, blocks, half, block), BF16),
-        scratch_shapes=resid_scratch + ring,
+        in_specs=[ANY] * 5,
+        out_specs=[VMEM, ANY],
+        out_shape=[jax.ShapeDtypeStruct((2, blocks, half, block), BF16), jax.ShapeDtypeStruct((rows, ff), BF16)],
+        scratch_shapes=[
+            pltpu.VMEM(w_b.shape, BF16), pltpu.VMEM((shard, width), BF16),
+            pltpu.SemaphoreType.DMA((tiles, 2)), pltpu.SemaphoreType.DMA((2,)), pltpu.SemaphoreType.DMA((2, 2)),
+        ] + resid_scratch + ring_scratch(n, half, depth, block, blocks, 1),
         compiler_params=pltpu.CompilerParams(collective_id=2, **params),
         cost_estimate=cost(2 * rows * depth * part * 2, 2 * (rows * depth + depth * part)),
-    )(act_a, act_b, w_first, resid)
+    )(normed, w_b, act_a, w_first, resid)
+    ring = ring_scratch(n, half, depth, block, blocks, 2)
     return pl.pallas_call(
         functools.partial(down_kernel, n),
         in_specs=[ANY] * 5,
@@ -586,7 +649,7 @@
         kv_heads = w_key.shape[1]
         rows = n_seqs * tokens
         local = w_query.shape[0]
-        ff_a = w_gate.shape[1] * 9 // 14 // 256 * 256
+        ff_a = w_gate.shape[1] * 10 // 14 // 256 * 256
         x = hidden.reshape(rows, d_model)
 
         w_qkv = jnp.concatenate([w.reshape(local, -1) for w in (w_query, w_key, w_value)], axis=1)
@@ -612,8 +675,8 @@
         mixed = attention(q, kv, kv_peer, n_seqs, kv_heads, heads // kv_heads, head)
         resid, normed_mlp = out_project(n_tp, mixed, full_out, x, mlp_gain.reshape(1, d_model))
         all_normed, act_a = gather_gate(n_tp, normed_mlp, full_a)
-        act_b = gate_up(all_normed, full_b, rows // n_tp)
-        y = down_project(n_tp, act_a, act_b, full_down0, full_down1, resid, full_down0.shape[1] // down_half)
+        y = down_project(n_tp, all_normed, full_b, act_a, full_down0, full_down1, resid, full_down0.shape[1] // down_half)
+        y = plain_copy(y, rows // 16)
         return y.reshape(hidden.shape)
 
     return jax.shard_map(

time: 913 us -> 903 us (0.989)
  local copies, waits for them, and re-layouts: 27.9 us -> 10.9 us
    unnamed x6 -> x5, local copies, waits for them, and re-layouts: 18.3 us -> 1.5 us
  transfers between devices with their start and end apart: 7 -> 7, of which waited for: 1 -> 1; matrix products, arithmetic and copies ran while one was open for 5% -> 5% of each run, Pallas kernels for 63% -> 62%
where the time goes in v2:
time: 903 us; the launch traced here: 892 us
  Pallas kernels  804 us (89%)
  other arithmetic  39.5 us (4%)
  waiting for transfers between devices  22.4 us (2%)
  between operations  13.8 us (2%)
  local copies, waits for them, and re-layouts  10.9 us (1%)
    pallas_call x1, Pallas kernels, down_project(): pl.pallas_call(functools.partial(down_kernel, n), in_specs=[ANY] * 5, out...  233 us
    pallas_call x1, Pallas kernels, out_project(): pl.pallas_call(functools.partial(out_kernel, n), in_specs=[ANY, ANY, ANY,...  170 us
    pallas_call x1, Pallas kernels, gather_gate(): pl.pallas_call(functools.partial(gather_gate_kernel, n, pieces), in_specs...  167 us
    pallas_call x1, Pallas kernels, down_project(): pl.pallas_call(functools.partial(down_sum_kernel, n), in_specs=[ANY] * 5,...  139 us
    pallas_call x2, Pallas kernels, project(): pl.pallas_call(functools.partial(proj_kernel, rope_heads, head), grid=(ro...  45.4 us
    pallas_call x1, Pallas kernels, attention(): pl.pallas_call(functools.partial(attn_kernel, group, head, tokens // 2),...  31.6 us
    all_gather x6, waiting for transfers between devices, gather(): return lax.all_gather(shard, GROUP_AXES, axis=axis, tiled=True)  21.4 us
    convert_element_type x1, other arithmetic, rms_norm(): return (hidden_f32 * lax.rsqrt(mean_sq + NORM_EPS) * gain).astype(BF16)  18.9 us
  transfers between devices with their start and end apart: 7, of which 1 were waited for; matrix products, arithmetic and copies ran while one was open for 5% of the time, Pallas kernels for 62%

profile of v2, /device:TPU:97, one launch (start us, length us, event | category | flops | bytes accessed | tf_op | source)
XLA Modules:
  0.0 891.6 jit_solution(6477351350559788017)
XLA Ops:
  6.5 0.0 all-gather.7.cloned.1.call-start
  6.6 1.5 copy.18
  8.0 1.1 copy_bitcast_fusion.1
  9.2 1.2 pad_maximum_fusion.2
  10.4 0.1 all-gather.7.cloned.1.call-update
  10.5 0.1 all-gather.9.cloned.1.call-start
  10.5 0.7 all-gather.9.cloned.1.call-update
  11.3 0.1 all-gather.11.cloned.1.call-start
  11.3 0.0 slice-start
  11.4 0.0 slice-start.2
  11.4 1.7 slice-done
  13.1 0.8 slice-done.2
  13.9 3.1 pad_maximum_fusion
  16.9 0.1 all-gather.11.cloned.1.call-update
  17.0 0.1 all-gather.15.cloned.1.call-start
  17.1 4.1 fusion.1
  21.2 0.0 slice-start.1
  21.2 0.0 slice-start.3
  21.2 0.1 all-gather.15.cloned.1.call-update
  21.3 0.1 all-gather.13.cloned.1.call-start
  21.3 1.2 slice-done.1
  22.5 0.5 slice-done.3
  23.0 0.0 copy-start.1
  23.0 1.5 pad_maximum_fusion.1
  24.5 0.1 all-gather.13.cloned.1.call-update
  24.6 0.1 all-gather.17.cloned.1.call-start
  24.7 0.0 copy-done.1
  24.7 8.4 multiply_reduce_fusion
  33.2 4.2 fusion
  37.4 0.0 copy-start
  37.4 2.1 pad_maximum_fusion.3
  39.5 0.0 copy-done
  39.5 18.9 %multiply_convert_fusion.x_ref = bf16[2304,4096]{1,0:T(8,128)(2,1)} fusion(f32[4096]{0:T(1024)S(1)} %copy-done, f32[2304]{0:T(1024)S(1)} %rsqrt.12, bf16[3,768,4096]{2,1,0:T(8,128)(2,1)} %param.11), kind=kLoop, calls=%fused_computation | loop fusion | flops 37748736 | bytes 37774336 | tf_op jit(solution)/shard_map/convert_element_type | solution.py:25
  58.4 21.3 %all-gather.7.cloned.1.call-done.w_ref = bf16[4096,1536]{1,0:T(8,128)(2,1)} async-done(((bf16[512,1536]{1,0:T(8,128)(2,1)}), bf16[4096,1536]{1,0:T(8,128)(2,1)}) %all-gather.7.cloned.1.call-update) | async-done | bytes 12582928 | tf_op jit(solution)/shard_map/all_gather | solution.py:632
  79.7 17.7 %shard_map.110.ko_ref.vo_ref = bf16[2304,512]{1,0:T(8,128)(2,1)} custom-call(bf16[2304,4096]{1,0:T(8,128)(2,1)} %multiply_convert_fusion.x_ref, bf16[4096,1536]{1,0:T(8,128)(2,1)} %all-gather.7.cloned.1.call-done.w_ref, f32[2304,128]{1,0:T(8,128)} %get-tuple-element.24.cos_ref, f32[2304,128]{1,0:T(8,128)} %get-tuple-element.25.sin_ref), custom_call_target="tpu_custom_call" | custom-call | flops 9663676416 | bytes 25427968 | tf_op jit(solution)/shard_map/pallas_call | solution.py:45
  97.4 0.3 collective-permute-start
  97.7 0.1 all-gather.17.cloned.1.call-update
  97.7 27.6 %shard_map.109.q_ref = bf16[2304,1024]{1,0:T(8,128)(2,1)} custom-call(bf16[2304,4096]{1,0:T(8,128)(2,1)} %multiply_convert_fusion.x_ref, bf16[4096,1536]{1,0:T(8,128)(2,1)} %all-gather.7.cloned.1.call-done.w_ref, f32[2304,128]{1,0:T(8,128)} %get-tuple-element.24.cos_ref, f32[2304,128]{1,0:T(8,128)} %get-tuple-element.25.sin_ref), custom_call_target="tpu_custom_call" | custom-call | flops 19327352832 | bytes 31981568 | tf_op jit(solution)/shard_map/pallas_call | solution.py:45
  125.3 0.0 collective-permute-done.kp_ref.vp_ref
  125.3 31.6 %shard_map.111.o_ref = bf16[2304,1024]{1,0:T(8,128)(2,1)} custom-call(bf16[2304,1024]{1,0:T(8,128)(2,1)} %shard_map.109.q_ref, bf16[2304,512]{1,0:T(8,128)(2,1)} %shard_map.110.ko_ref.vo_ref, bf16[2304,512]{1,0:T(8,128)(2,1)} %shard_map.110.ko_ref.vo_ref, bf16[2304,512]{1,0:T(8,128)(2,1)} %collective-permute-done.kp_ref.vp_ref, ...), custom_call_target="tpu_custom_call" | custom-call | flops 18119393280 | bytes 9437184 | tf_op jit(solution)/shard_map/pallas_call | solution.py:105
  156.9 0.0 all-gather.9.cloned.1.call-done.w_ref
  156.9 170.3 %shard_map.112 = (bf16[576,4096]{1,0:T(8,128)(2,1)}, bf16[576,4096]{1,0:T(8,128)(2,1)}) custom-call(bf16[2304,1024]{1,0:T(8,128)(2,1)} %shard_map.111.o_ref, bf16[1024,4096]{1,0:T(8,128)(2,1)} %all-gather.9.cloned.1.call-done.w_ref, bf16[2304,4096]{1,0:T(8,128)(2,1)} %bitcast.15, f32[1,4096]{1,0:T(1,128)} %bitcast.21), custom_call_target="tpu_custom_call" | custom-call | flops 96636764160 | bytes 13107200 | tf_op jit(solution)/shard_map/pallas_call | solution.py:255
  327.3 0.0 all-gather.11.cloned.1.call-done.w_ref
  327.3 167.3 %shard_map.113 = (bf16[2304,4096]{1,0:T(8,128)(2,1)}, bf16[2304,2560]{1,0:T(8,128)(2,1)}) custom-call(bf16[576,4096]{1,0:T(8,128)(2,1)} %get-tuple-element.11.b_ref, bf16[4096,5120]{1,0:T(8,128)(2,1)} %all-gather.11.cloned.1.call-done.w_ref), custom_call_target="tpu_custom_call" | custom-call | flops 193273528320 | bytes 60817408 | tf_op jit(solution)/shard_map/pallas_call | solution.py:387
  494.6 0.0 all-gather.15.cloned.1.call-done.w_ref
  494.7 0.0 all-gather.13.cloned.1.call-done.wb_ref
  494.7 138.5 %shard_map.114 = (bf16[2,8,288,256]{3,2,1,0:T(8,128)(2,1)}, bf16[2304,1024]{1,0:T(8,128)(2,1)}) custom-call(bf16[2304,4096]{1,0:T(8,128)(2,1)} %get-tuple-element.13.x_ref, bf16[4096,2048]{1,0:T(8,128)(2,1)} %all-gather.13.cloned.1.call-done.wb_ref, bf16[2304,2560]{1,0:T(8,128)(2,1)} %get-tuple-element.12.ua_ref, ...), custom_call_target="tpu_custom_call" | custom-call | flops 67645734912 | bytes 31195136 | tf_op jit(solution)/shard_map/pallas_call | solution.py:604
  633.2 0.0 all-gather.17.cloned.1.call-done.w_ref
  633.3 232.7 %shard_map.115.x_ref = bf16[2304,4096]{1,0:T(8,128)(2,1)} custom-call(bf16[2304,2560]{1,0:T(8,128)(2,1)} %get-tuple-element.12.ua_ref, bf16[2304,1024]{1,0:T(8,128)(2,1)} %get-tuple-element.15.ub_ref, bf16[3584,2048]{1,0:T(8,128)(2,1)} %all-gather.17.cloned.1.call-done.w_ref, bf16[576,4096]{1,0:T(8,128)(2,1)} %get-tuple-element.14.r_ref, ...), custom_call_target="tpu_custom_call" | custom-call | flops 202937204736 | bytes 31195136 | tf_op jit(solution)/shard_map/pallas_call | solution.py:617
  866.0 18.6 %shard_map.116 = bf16[2304,4096]{1,0:T(8,128)(2,1)} custom-call(bf16[2304,4096]{1,0:T(8,128)(2,1)} %shard_map.115.x_ref), custom_call_target="tpu_custom_call" | custom-call | flops 1000 | bytes 37748736 | tf_op jit(solution)/shard_map/pallas_call | solution.py:414
  (5 shorter events, 0.1 us)
Async XLA Ops:
  6.5 73.1 %all-gather.7.cloned.1.call-start = ((), (), s32[]{:S(2)}) async-start(), calls=%async_computation | async-start | bytes 14155776 | tf_op jit(solution)/shard_map/all_gather | solution.py:632
  10.5 146.5 %all-gather.9.cloned.1.call-start = ((), (), s32[]{:S(2)}) async-start(), calls=%async_computation.1 | async-start | bytes 9437184 | tf_op jit(solution)/shard_map/all_gather | solution.py:632
  11.3 316.0 %all-gather.11.cloned.1.call-start = ((), (), s32[]{:S(2)}) async-start(), calls=%async_computation.2 | async-start | bytes 47185920 | tf_op jit(solution)/shard_map/all_gather | solution.py:632
  11.3 1.7 slice-start
  11.4 2.5 slice-start.2
  17.0 477.7 %all-gather.15.cloned.1.call-start = ((), (), s32[]{:S(2)}) async-start(), calls=%async_computation.4 | async-start | bytes 16515072 | tf_op jit(solution)/shard_map/all_gather | solution.py:632
  21.2 1.4 slice-start.1
  21.2 1.8 slice-start.3
  21.3 473.4 %all-gather.13.cloned.1.call-start = ((), (), s32[]{:S(2)}) async-start(), calls=%async_computation.3 | async-start | bytes 18874368 | tf_op jit(solution)/shard_map/all_gather | solution.py:632
  23.0 1.7 copy-start.1
  24.6 608.7 %all-gather.17.cloned.1.call-start = ((), (), s32[]{:S(2)}) async-start(), calls=%async_computation.5 | async-start | bytes 16515072 | tf_op jit(solution)/shard_map/all_gather | solution.py:632
  37.4 2.1 copy-start
  97.4 27.9 %collective-permute-start = (bf16[2304,512]{1,0:T(8,128)(2,1)}, bf16[2304,512]{1,0:T(8,128)(2,1)}, u32[]{:S(2)}, u32[]{:S(2)}) collective-permute-start(bf16[2304,512]{1,0:T(8,128)(2,1)} %shard_map.110.ko_ref.vo_ref), channel_id=1, source_target_pairs={{0,1},{1,0},{2,3},{3,2},{4,5},{5,4},{6,7},{7,6},{8,9},{9,8},{10,11... | collective-permute-start | bytes 7077896 | tf_op jit(solution)/shard_map/ppermute | solution.py:673
Sparse Core Ops, SparseCore 0:
  10.6 69.0 all-gather.6
  81.3 47.4 all-gather.8
  130.4 190.1 all-gather.10
  322.1 77.4 all-gather.14
  401.0 83.5 all-gather.12
  486.0 78.7 all-gather.16

commit v3 on v2

--- a/solution.py
+++ b/solution.py
@@ -130,7 +130,7 @@
 
 
 def ring_matmul_scatter(n, me, sides, u_refs, w_ref, u_buf, w_buf, s_buf, r_buf, u_sem, w_sem, send_sem, recv_sem, finish, hook=None, prepare=None):
-    half = u_buf.shape[2]
+    half = u_buf.shape[1] // 2
     block = w_buf.shape[2]
     blocks = w_ref.shape[1] // block
 
@@ -141,7 +141,7 @@
             at = 0
             for i, u_ref in enumerate(u_refs):
                 copies.append(pltpu.make_async_copy(
-                    u_ref.at[pl.ds(row, half), :], u_buf.at[step % 2, d, :, pl.ds(at, u_ref.shape[1])], u_sem.at[step % 2, d, i]))
+                    u_ref.at[pl.ds(row, half), :], u_buf.at[step % 2, pl.ds(d * half, half), pl.ds(at, u_ref.shape[1])], u_sem.at[step % 2, d, i]))
                 at += u_ref.shape[1]
         return copies
 
@@ -175,9 +175,9 @@
                 @pl.when(cb + 1 < blocks)
                 def _():
                     w_copy(cb + 1, 1 - slot).start()
-            parts = [jnp.dot(u_buf[step % 2, d], w_buf[slot], preferred_element_type=F32) for d in range(2)]
+            both = jnp.dot(u_buf[step % 2], w_buf[slot], preferred_element_type=F32)
             for d in range(2):
-                part = parts[d]
+                part = both[d * half:(d + 1) * half]
                 if step > 0:
                     send(step - 1, d, cb).wait_recv()
                     part = part + r_buf[step - 1, d, cb].astype(F32)
@@ -206,7 +206,7 @@
 
 def ring_scratch(n, half, depth, block, blocks, n_u):
     return [
-        pltpu.VMEM((2, 2, half, depth), BF16),
+        pltpu.VMEM((2, 2 * half, depth), BF16),
         pltpu.VMEM((2, depth, block), BF16),
         pltpu.VMEM((2, blocks, half, block), BF16),
         pltpu.VMEM((n - 1, 2, blocks, half, block), BF16),
@@ -405,14 +405,38 @@
     )(b, w)
 
 
-def copy_kernel(x_ref, o_ref):
-    o_ref[...] = x_ref[...]
-
-
-def plain_copy(x, tile):
-    spec = pl.BlockSpec((tile, x.shape[1]), lambda i: (i, 0))
+def copy_kernel(x_ref, o_ref, buf, in_sem, out_sem):
+    pieces, tile, _ = buf.shape
+
+    def load(i):
+        return pltpu.make_async_copy(x_ref.at[pl.ds(pl.multiple_of(i * tile, tile), tile), :], buf.at[i], in_sem.at[i])
+
+    def store(i):
+        return pltpu.make_async_copy(buf.at[i], o_ref.at[pl.ds(pl.multiple_of(i * tile, tile), tile), :], out_sem.at[i])
+
+    def begin(i, _):
+        load(i).start()
+        return 0
+
+    def turn(i, _):
+        load(i).wait()
+        store(i).start()
+        return 0
+
+    def end(i, _):
+        store(i).wait()
+        return 0
+
+    for step in (begin, turn, end):
+        lax.fori_loop(0, pieces, step, 0)
+
+
+def plain_copy(x, pieces):
+    rows, width = x.shape
     return pl.pallas_call(
-        copy_kernel, grid=(x.shape[0] // tile,), in_specs=[spec], out_specs=spec, out_shape=jax.ShapeDtypeStruct(x.shape, x.dtype),
+        copy_kernel, in_specs=[ANY], out_specs=ANY, out_shape=jax.ShapeDtypeStruct(x.shape, x.dtype),
+        scratch_shapes=[pltpu.VMEM((pieces, rows // pieces, width), x.dtype), pltpu.SemaphoreType.DMA((pieces,)), pltpu.SemaphoreType.DMA((pieces,))],
+        compiler_params=pltpu.CompilerParams(vmem_limit_bytes=VMEM_LIMIT),
         cost_estimate=cost(1000, 4 * x.size))(x)
 
 
@@ -460,7 +484,7 @@
 
     def ub_copies(step):
         return [pltpu.make_async_copy(
-            u_buf.at[step % 2, d, :, pl.ds(ff_a, ff)], ub_ref.at[rows_of(d, step), :], ub_sem.at[step % 2, d]) for d in range(2)]
+            u_buf.at[step % 2, pl.ds(d * half, half), pl.ds(ff_a, ff)], ub_ref.at[rows_of(d, step), :], ub_sem.at[step % 2, d]) for d in range(2)]
 
     for c in x_copies(0):
         c.start()
@@ -486,10 +510,8 @@
                 for c in wb_copies(t):
                     c.wait()
             at = pl.multiple_of(t * tile, tile)
-            act = gated(x_buf[...], wb_buf[:, pl.ds(at, tile)], wb_buf[:, pl.ds(ff + at, tile)])
             to = pl.ds(pl.multiple_of(ff_a + t * tile, tile), tile)
-            for d in range(2):
-                u_buf[step % 2, d, :, to] = act[d * half:(d + 1) * half, :]
+            u_buf[step % 2, :, to] = gated(x_buf[...], wb_buf[:, pl.ds(at, tile)], wb_buf[:, pl.ds(ff + at, tile)])
             return 0
 
         lax.fori_loop(0, tiles, one_tile, 0)
@@ -676,7 +698,7 @@
         resid, normed_mlp = out_project(n_tp, mixed, full_out, x, mlp_gain.reshape(1, d_model))
         all_normed, act_a = gather_gate(n_tp, normed_mlp, full_a)
         y = down_project(n_tp, all_normed, full_b, act_a, full_down0, full_down1, resid, full_down0.shape[1] // down_half)
-        y = plain_copy(y, rows // 16)
+        y = plain_copy(y, 24)
         return y.reshape(hidden.shape)
 
     return jax.shard_map(

time: 903 us -> 868 us (0.961)
  Pallas kernels: 804 us -> 770 us
    pallas_call x1, Pallas kernels: 139 us -> 110 us  [down_project(): pl.pallas_call(functools.partial(down_sum_kernel, n), in_specs=[ANY] * 5,...]
  transfers between devices with their start and end apart: 7 -> 7, of which waited for: 1 -> 1; matrix products, arithmetic and copies ran while one was open for 5% -> 5% of each run, Pallas kernels for 62% -> 61%
where the time goes in v3:
time: 868 us; the launch traced here: 857 us
  Pallas kernels  770 us (89%)
  other arithmetic  39.5 us (5%)
  waiting for transfers between devices  22.4 us (3%)
  between operations  13.9 us (2%)
  local copies, waits for them, and re-layouts  10.9 us (1%)
    pallas_call x1, Pallas kernels, down_project(): pl.pallas_call(functools.partial(down_kernel, n), in_specs=[ANY] * 5, out...  233 us
    pallas_call x1, Pallas kernels, out_project(): pl.pallas_call(functools.partial(out_kernel, n), in_specs=[ANY, ANY, ANY,...  170 us
    pallas_call x1, Pallas kernels, gather_gate(): pl.pallas_call(functools.partial(gather_gate_kernel, n, pieces), in_specs...  167 us
    pallas_call x1, Pallas kernels, down_project(): pl.pallas_call(functools.partial(down_sum_kernel, n), in_specs=[ANY] * 5,...  110 us
    pallas_call x2, Pallas kernels, project(): pl.pallas_call(functools.partial(proj_kernel, rope_heads, head), grid=(ro...  45.4 us
    pallas_call x1, Pallas kernels, attention(): pl.pallas_call(functools.partial(attn_kernel, group, head, tokens // 2),...  31.6 us
    all_gather x6, waiting for transfers between devices, gather(): return lax.all_gather(shard, GROUP_AXES, axis=axis, tiled=True)  21.4 us
    convert_element_type x1, other arithmetic, rms_norm(): return (hidden_f32 * lax.rsqrt(mean_sq + NORM_EPS) * gain).astype(BF16)  18.9 us
  transfers between devices with their start and end apart: 7, of which 1 were waited for; matrix products, arithmetic and copies ran while one was open for 5% of the time, Pallas kernels for 61%

profile of v3, /device:TPU:97, one launch (start us, length us, event | category | flops | bytes accessed | tf_op | source)
XLA Modules:
  0.0 857.4 jit_solution(15976768606613190341)
XLA Ops:
  6.5 0.0 all-gather.7.cloned.1.call-start
  6.6 1.5 copy.18
  8.0 1.1 copy_bitcast_fusion.1
  9.2 1.2 pad_maximum_fusion.2
  10.4 0.1 all-gather.7.cloned.1.call-update
  10.5 0.1 all-gather.9.cloned.1.call-start
  10.5 0.7 all-gather.9.cloned.1.call-update
  11.3 0.1 all-gather.11.cloned.1.call-start
  11.3 0.0 slice-start
  11.4 0.0 slice-start.2
  11.4 1.7 slice-done
  13.1 0.8 slice-done.2
  13.9 3.1 pad_maximum_fusion
  16.9 0.1 all-gather.11.cloned.1.call-update
  17.0 0.1 all-gather.15.cloned.1.call-start
  17.1 4.1 fusion.1
  21.2 0.0 slice-start.1
  21.2 0.0 slice-start.3
  21.2 0.1 all-gather.15.cloned.1.call-update
  21.3 0.1 all-gather.13.cloned.1.call-start
  21.3 1.2 slice-done.1
  22.5 0.5 slice-done.3
  23.0 0.0 copy-start.1
  23.0 1.5 pad_maximum_fusion.1
  24.5 0.1 all-gather.13.cloned.1.call-update
  24.6 0.1 all-gather.17.cloned.1.call-start
  24.7 0.0 copy-done.1
  24.7 8.4 multiply_reduce_fusion
  33.2 4.2 fusion
  37.4 0.0 copy-start
  37.4 2.1 pad_maximum_fusion.3
  39.5 0.0 copy-done
  39.5 18.9 %multiply_convert_fusion.x_ref = bf16[2304,4096]{1,0:T(8,128)(2,1)} fusion(f32[4096]{0:T(1024)S(1)} %copy-done, f32[2304]{0:T(1024)S(1)} %rsqrt.12, bf16[3,768,4096]{2,1,0:T(8,128)(2,1)} %param.11), kind=kLoop, calls=%fused_computation | loop fusion | flops 37748736 | bytes 37774336 | tf_op jit(solution)/shard_map/convert_element_type | solution.py:25
  58.4 21.3 %all-gather.7.cloned.1.call-done.w_ref = bf16[4096,1536]{1,0:T(8,128)(2,1)} async-done(((bf16[512,1536]{1,0:T(8,128)(2,1)}), bf16[4096,1536]{1,0:T(8,128)(2,1)}) %all-gather.7.cloned.1.call-update) | async-done | bytes 12582928 | tf_op jit(solution)/shard_map/all_gather | solution.py:654
  79.7 17.7 %shard_map.110.ko_ref.vo_ref = bf16[2304,512]{1,0:T(8,128)(2,1)} custom-call(bf16[2304,4096]{1,0:T(8,128)(2,1)} %multiply_convert_fusion.x_ref, bf16[4096,1536]{1,0:T(8,128)(2,1)} %all-gather.7.cloned.1.call-done.w_ref, f32[2304,128]{1,0:T(8,128)} %get-tuple-element.24.cos_ref, f32[2304,128]{1,0:T(8,128)} %get-tuple-element.25.sin_ref), custom_call_target="tpu_custom_call" | custom-call | flops 9663676416 | bytes 25427968 | tf_op jit(solution)/shard_map/pallas_call | solution.py:45
  97.4 0.3 collective-permute-start
  97.7 0.1 all-gather.17.cloned.1.call-update
  97.7 27.6 %shard_map.109.q_ref = bf16[2304,1024]{1,0:T(8,128)(2,1)} custom-call(bf16[2304,4096]{1,0:T(8,128)(2,1)} %multiply_convert_fusion.x_ref, bf16[4096,1536]{1,0:T(8,128)(2,1)} %all-gather.7.cloned.1.call-done.w_ref, f32[2304,128]{1,0:T(8,128)} %get-tuple-element.24.cos_ref, f32[2304,128]{1,0:T(8,128)} %get-tuple-element.25.sin_ref), custom_call_target="tpu_custom_call" | custom-call | flops 19327352832 | bytes 31981568 | tf_op jit(solution)/shard_map/pallas_call | solution.py:45
  125.3 0.0 collective-permute-done.kp_ref.vp_ref
  125.3 31.6 %shard_map.111.o_ref = bf16[2304,1024]{1,0:T(8,128)(2,1)} custom-call(bf16[2304,1024]{1,0:T(8,128)(2,1)} %shard_map.109.q_ref, bf16[2304,512]{1,0:T(8,128)(2,1)} %shard_map.110.ko_ref.vo_ref, bf16[2304,512]{1,0:T(8,128)(2,1)} %shard_map.110.ko_ref.vo_ref, bf16[2304,512]{1,0:T(8,128)(2,1)} %collective-permute-done.kp_ref.vp_ref, ...), custom_call_target="tpu_custom_call" | custom-call | flops 18119393280 | bytes 9437184 | tf_op jit(solution)/shard_map/pallas_call | solution.py:105
  156.9 0.0 all-gather.9.cloned.1.call-done.w_ref
  156.9 169.6 %shard_map.112 = (bf16[576,4096]{1,0:T(8,128)(2,1)}, bf16[576,4096]{1,0:T(8,128)(2,1)}) custom-call(bf16[2304,1024]{1,0:T(8,128)(2,1)} %shard_map.111.o_ref, bf16[1024,4096]{1,0:T(8,128)(2,1)} %all-gather.9.cloned.1.call-done.w_ref, bf16[2304,4096]{1,0:T(8,128)(2,1)} %bitcast.15, f32[1,4096]{1,0:T(1,128)} %bitcast.21), custom_call_target="tpu_custom_call" | custom-call | flops 96636764160 | bytes 13107200 | tf_op jit(solution)/shard_map/pallas_call | solution.py:255
  326.5 0.0 all-gather.11.cloned.1.call-done.w_ref
  326.6 167.4 %shard_map.113 = (bf16[2304,4096]{1,0:T(8,128)(2,1)}, bf16[2304,2560]{1,0:T(8,128)(2,1)}) custom-call(bf16[576,4096]{1,0:T(8,128)(2,1)} %get-tuple-element.11.b_ref, bf16[4096,5120]{1,0:T(8,128)(2,1)} %all-gather.11.cloned.1.call-done.w_ref), custom_call_target="tpu_custom_call" | custom-call | flops 193273528320 | bytes 60817408 | tf_op jit(solution)/shard_map/pallas_call | solution.py:387
  494.0 0.0 all-gather.15.cloned.1.call-done.w_ref
  494.0 0.0 all-gather.13.cloned.1.call-done.wb_ref
  494.0 109.8 %shard_map.114 = (bf16[2,8,288,256]{3,2,1,0:T(8,128)(2,1)}, bf16[2304,1024]{1,0:T(8,128)(2,1)}) custom-call(bf16[2304,4096]{1,0:T(8,128)(2,1)} %get-tuple-element.13.x_ref, bf16[4096,2048]{1,0:T(8,128)(2,1)} %all-gather.13.cloned.1.call-done.wb_ref, bf16[2304,2560]{1,0:T(8,128)(2,1)} %get-tuple-element.12.ua_ref, ...), custom_call_target="tpu_custom_call" | custom-call | flops 67645734912 | bytes 31195136 | tf_op jit(solution)/shard_map/pallas_call | solution.py:626
  603.8 0.0 all-gather.17.cloned.1.call-done.w_ref
  603.8 233.2 %shard_map.115.x_ref = bf16[2304,4096]{1,0:T(8,128)(2,1)} custom-call(bf16[2304,2560]{1,0:T(8,128)(2,1)} %get-tuple-element.12.ua_ref, bf16[2304,1024]{1,0:T(8,128)(2,1)} %get-tuple-element.15.ub_ref, bf16[3584,2048]{1,0:T(8,128)(2,1)} %all-gather.17.cloned.1.call-done.w_ref, bf16[576,4096]{1,0:T(8,128)(2,1)} %get-tuple-element.14.r_ref, ...), custom_call_target="tpu_custom_call" | custom-call | flops 202937204736 | bytes 31195136 | tf_op jit(solution)/shard_map/pallas_call | solution.py:639
  837.0 13.4 %shard_map.116 = bf16[2304,4096]{1,0:T(8,128)(2,1)} custom-call(bf16[2304,4096]{1,0:T(8,128)(2,1)} %shard_map.115.x_ref), custom_call_target="tpu_custom_call" | custom-call | flops 1000 | bytes 37748736 | tf_op jit(solution)/shard_map/pallas_call | solution.py:436
  (5 shorter events, 0.1 us)
Async XLA Ops:
  6.5 73.1 %all-gather.7.cloned.1.call-start = ((), (), s32[]{:S(2)}) async-start(), calls=%async_computation | async-start | bytes 14155776 | tf_op jit(solution)/shard_map/all_gather | solution.py:654
  10.5 146.5 %all-gather.9.cloned.1.call-start = ((), (), s32[]{:S(2)}) async-start(), calls=%async_computation.1 | async-start | bytes 9437184 | tf_op jit(solution)/shard_map/all_gather | solution.py:654
  11.3 315.3 %all-gather.11.cloned.1.call-start = ((), (), s32[]{:S(2)}) async-start(), calls=%async_computation.2 | async-start | bytes 47185920 | tf_op jit(solution)/shard_map/all_gather | solution.py:654
  11.3 1.7 slice-start
  11.4 2.5 slice-start.2
  17.0 477.0 %all-gather.15.cloned.1.call-start = ((), (), s32[]{:S(2)}) async-start(), calls=%async_computation.4 | async-start | bytes 16515072 | tf_op jit(solution)/shard_map/all_gather | solution.py:654
  21.2 1.4 slice-start.1
  21.2 1.8 slice-start.3
  21.3 472.8 %all-gather.13.cloned.1.call-start = ((), (), s32[]{:S(2)}) async-start(), calls=%async_computation.3 | async-start | bytes 18874368 | tf_op jit(solution)/shard_map/all_gather | solution.py:654
  23.0 1.7 copy-start.1
  24.6 579.2 %all-gather.17.cloned.1.call-start = ((), (), s32[]{:S(2)}) async-start(), calls=%async_computation.5 | async-start | bytes 16515072 | tf_op jit(solution)/shard_map/all_gather | solution.py:654
  37.4 2.1 copy-start
  97.4 27.9 %collective-permute-start = (bf16[2304,512]{1,0:T(8,128)(2,1)}, bf16[2304,512]{1,0:T(8,128)(2,1)}, u32[]{:S(2)}, u32[]{:S(2)}) collective-permute-start(bf16[2304,512]{1,0:T(8,128)(2,1)} %shard_map.110.ko_ref.vo_ref), channel_id=1, source_target_pairs={{0,1},{1,0},{2,3},{3,2},{4,5},{5,4},{6,7},{7,6},{8,9},{9,8},{10,11... | collective-permute-start | bytes 7077896 | tf_op jit(solution)/shard_map/ppermute | solution.py:695
Sparse Core Ops, SparseCore 0:
  10.6 69.0 all-gather.6
  81.3 47.4 all-gather.8
  130.4 190.2 all-gather.10
  322.1 77.4 all-gather.14
  401.1 83.2 all-gather.12
  485.8 78.7 all-gather.16
